TPU v7x, 32 devices: a whole 2x2x4 slice. The times are simulated.
32 devices in a mesh: cp: 8 (over z, x), tp: 4 (over y, core).
Axes of the slice: x: 2, y: 2, z: 4, core: 2. Of those that a mesh axis runs over, the one named last changes fastest.
Arguments:
- queries: bfloat16 [1536, 2048], P('cp', 'tp'), may hold values from -128 to 128
- keys: bfloat16 [1536, 256], P('cp'), may hold values from -6 to 6
- values: bfloat16 [1536, 256], P('cp'), may hold values from -6 to 6
- positions: int32 [1536], replicated, may hold values from 0 to 1535, as said below
- out_weight: bfloat16 [2048, 8192], P('tp'), may hold values from -0.125 to 0.125
Outputs:
- mixed: bfloat16 [1536, 8192], P(('cp', 'tp'))
Inputs may be any that keep to these rules, and one draw needn't show every extreme that they name: positions is a permutation of 0 to 1535. The tokens stored at indices d * 192 to (d + 1) * 192 - 1 form two runs of 96 consecutive positions, the first starting at b * 96 and the second at (15 - b) * 96 for some b, each b used by one d.
All inputs are finite; a program needn't handle non-finite values.
Results may differ from a plain program's by a relative error of at most 0.013.
Values may be sent and summed in bfloat16 or wider, within the bound.
No kernel may reach another device: no remote copies, remote signals or barrier semaphores. Data moves between devices by JAX's collectives and lax.ppermute only.
A program may use at most 128 MiB of HBM per device.

v0:
```python
import functools

import jax
import jax.numpy as jnp
from jax import lax
from jax.experimental import pallas as pl
from jax.experimental.pallas import tpu as pltpu
from jax.sharding import PartitionSpec as P


HEAD = 128
GROUP = 8
NEG = -1e30
LOG2E = 1.4426950408889634
AXES = ("cp", "tp")
VMEM_LIMIT = 36 * 2**20
COLUMN_CUTS = (0, 4, 10, 16)
TILE = 512


def project(attended, weight, keep_ref, send_ref):
    partial = jnp.dot(attended, weight, preferred_element_type=jnp.float32).astype(jnp.bfloat16)
    part = keep_ref.shape[0]
    keep_ref[...] = partial[:part]
    send_ref[...] = partial[part:]


def attention_kernel(stack, *refs):
    bias_ref, own_ref, sib_ref, own_w_ref, sib_w_ref = refs[:5]
    block_refs = refs[5:-5]
    attended_ref, keep_ref, send_ref, weight_ref, sems = refs[-5:]
    half, width = own_w_ref.shape[0], weight_ref.shape[1]
    loads = [
        pltpu.make_async_copy(
            ref.at[:, pl.ds(0, width)], weight_ref.at[pl.ds(i * half, half)], sems.at[i]
        )
        for i, ref in enumerate((own_w_ref, sib_w_ref))
    ]
    for load in loads:
        load.start()

    @pl.when(bias_ref[0, 0] <= 0.0)
    def _():
        keys = jnp.concatenate([r[:, :HEAD] for r in block_refs], axis=0)
        values = jnp.concatenate([r[:, HEAD:] for r in block_refs], axis=0)
        values = jnp.concatenate([values, jnp.ones_like(values)], axis=1)
        scale = HEAD ** (-0.5) * LOG2E
        rows = own_ref.shape[0]
        heads = own_ref.shape[1] // HEAD
        for side, q_ref in enumerate((own_ref, sib_ref)):
            for first in range(0, heads, stack):
                q = jnp.concatenate(
                    [q_ref[:, h * HEAD : (h + 1) * HEAD] for h in range(first, first + stack)], axis=0
                )
                scores = lax.dot_general(
                    q, keys, (((1,), (1,)), ((), ())), preferred_element_type=jnp.float32
                )
                scores = (scores.reshape(stack, rows, -1) + bias_ref[...][None]).reshape(scores.shape)
                top = jnp.max(scores, axis=1, keepdims=True)
                weights = jnp.exp2((scores - top) * scale).astype(jnp.bfloat16)
                mixed = jnp.dot(weights, values, preferred_element_type=jnp.float32)
                result = (mixed[:, :HEAD] / mixed[:, HEAD:]).astype(jnp.bfloat16)
                for i in range(stack):
                    at = (side * heads + first + i) * HEAD
                    attended_ref[:, at : at + HEAD] = result[i * rows : (i + 1) * rows]

    for load in loads:
        load.wait()
    project(attended_ref[...], weight_ref[...], keep_ref, send_ref)


def project_kernel(first, attended_ref, own_w_ref, sib_w_ref, keep_ref, send_ref, weight_ref, sems):
    half = own_w_ref.shape[0]
    tiles, _, tile = weight_ref.shape
    loads = [
        [
            pltpu.make_async_copy(
                ref.at[:, pl.ds(first + t * tile, tile)],
                weight_ref.at[t, pl.ds(i * half, half)],
                sems.at[t, i],
            )
            for i, ref in enumerate((own_w_ref, sib_w_ref))
        ]
        for t in range(tiles)
    ]
    for pair in loads:
        for load in pair:
            load.start()
    for t, pair in enumerate(loads):
        for load in pair:
            load.wait()
        cols = pl.ds(t * tile, tile)
        project(attended_ref[...], weight_ref[t], keep_ref.at[:, cols], send_ref.at[:, cols])


def finish_kernel(first, *refs):
    keep_ref, got_ref = refs[:2]
    out_ref, sum_ref, sem = refs[-3:]
    sum_ref[...] = (
        keep_ref[...].astype(jnp.float32) + got_ref[...].astype(jnp.float32)
    ).astype(jnp.bfloat16)
    store = pltpu.make_async_copy(
        sum_ref, out_ref.at[:, pl.ds(first, sum_ref.shape[1])], sem
    )
    store.start()
    store.wait()


def pairing(cp_size):
    low = [o for o in range(2, cp_size) if o < cp_size // 2]
    high = [o for o in range(2, cp_size) if o >= cp_size // 2]
    high = sorted(high, key=lambda o: (o & 1, -o))
    order = high + low
    return [(order[i], order[i + 1]) for i in range(0, len(order), 2)]


def shards(cp_size, tp_size, queries, keys, values, positions, out_weight):
    rows = queries.shape[0]
    heads = queries.shape[1] // HEAD
    part = rows // tp_size
    cp = lax.axis_index("cp")
    tp = lax.axis_index("tp")
    core = tp % 2

    def permute(x, to_cp, to_tp):
        pairs = [
            (c * tp_size + t, to_cp(c, t) * tp_size + to_tp(t))
            for c in range(cp_size)
            for t in range(tp_size)
        ]
        return lax.ppermute(x, AXES, pairs)

    def to_sibling(x):
        return permute(x, lambda c, t: c, lambda t: t ^ 1)

    kv_group = tp * heads // GROUP
    block = jnp.concatenate(
        [lax.dynamic_slice_in_dim(a, kv_group * HEAD, HEAD, 1) for a in (keys, values)], axis=1
    )
    blocks = [block]
    offsets = [(0, 0)]
    fetched = []
    for pair in pairing(cp_size):
        arrived = permute(block, lambda c, t, pair=pair: c ^ pair[t & 1], lambda t: t)
        fetched.append(arrived)
        blocks.append(arrived)
        offsets.append(pair)
    blocks.append(permute(block, lambda c, t: c ^ 1, lambda t: t))
    offsets.append((1, 1))
    for arrived, pair in zip(fetched, pairing(cp_size)):
        blocks.append(to_sibling(arrived))
        offsets.append((pair[1], pair[0]))

    def rows_of(x, c):
        return jnp.concatenate(
            [
                lax.dynamic_slice_in_dim(x, ((tp // 2 + s) % 2 * 2 + c) * part, part, 0)
                for s in (0, 1)
            ],
            axis=0,
        )

    own_q = rows_of(queries, core)
    sib_q = to_sibling(rows_of(queries, 1 - core))
    sib_weight = to_sibling(out_weight)

    query_pos = rows_of(lax.dynamic_slice_in_dim(positions, cp * rows, rows, 0), core)
    key_pos = jnp.concatenate(
        [
            lax.dynamic_slice_in_dim(positions, (cp ^ jnp.where(core == 0, a, b)) * rows, rows, 0)
            for a, b in offsets
        ]
    )
    bias = jnp.where(key_pos[None, :] <= query_pos[:, None], 0.0, NEG).astype(jnp.float32)

    width = out_weight.shape[1]
    cuts = [c * width // COLUMN_CUTS[-1] for c in COLUMN_CUTS]
    vmem = functools.partial(pltpu.with_memory_space_constraint, memory_space=pltpu.VMEM)
    hbm = pl.BlockSpec(memory_space=pltpu.HBM)
    weights = [pltpu.with_memory_space_constraint(w, pltpu.HBM) for w in (out_weight, sib_weight)]
    whole = pl.BlockSpec(memory_space=pltpu.VMEM)
    attended = None
    kept = []
    got = []
    for lo, hi in zip(cuts[:-1], cuts[1:]):
        half = pltpu.VMEM((part, hi - lo), jnp.bfloat16)
        if attended is None:
            stack = min(heads, max(1, 2 * 1536 // bias.shape[1]))
            attended, keep, send = pl.pallas_call(
                functools.partial(attention_kernel, stack),
                in_specs=[whole] * 3 + [hbm] * 2 + [whole] * len(blocks),
                out_shape=(pltpu.VMEM((2 * part, 2 * heads * HEAD), jnp.bfloat16), half, half),
                scratch_shapes=[
                    pltpu.VMEM((2 * heads * HEAD, hi - lo), jnp.bfloat16),
                    pltpu.SemaphoreType.DMA((2,)),
                ],
                compiler_params=pltpu.CompilerParams(vmem_limit_bytes=VMEM_LIMIT),
                name="attention",
            )(vmem(bias), vmem(own_q), vmem(sib_q), *weights, *[vmem(b) for b in blocks])
        else:
            keep, send = pl.pallas_call(
                functools.partial(project_kernel, lo),
                in_specs=[whole, hbm, hbm],
                out_shape=(half, half),
                scratch_shapes=[
                    pltpu.VMEM(((hi - lo) // TILE, 2 * heads * HEAD, TILE), jnp.bfloat16),
                    pltpu.SemaphoreType.DMA(((hi - lo) // TILE, 2)),
                ],
                compiler_params=pltpu.CompilerParams(vmem_limit_bytes=VMEM_LIMIT),
                name="project",
            )(attended, *weights)
        kept.append(keep)
        got.append(permute(send, lambda c, t: c, lambda t: t ^ 2))
    out = ()
    for lo, hi, keep, arrived in zip(cuts[:-1], cuts[1:], kept, got):
        out = pl.pallas_call(
            functools.partial(finish_kernel, lo),
            in_specs=[whole, whole] + [hbm] * len(out),
            out_specs=(hbm,),
            out_shape=(pltpu.HBM((part, width), jnp.bfloat16),),
            scratch_shapes=[pltpu.VMEM((part, hi - lo), jnp.bfloat16), pltpu.SemaphoreType.DMA],
            input_output_aliases={2: 0} if out else {},
            name="finish",
        )(vmem(keep), vmem(arrived), *out)
    return out[0]


def solution(mesh):
    in_specs = (P("cp", "tp"), P("cp", None), P("cp", None), P(), P("tp", None))
    out_specs = P(("cp", "tp"), None)
    cp_size, tp_size = mesh.shape["cp"], mesh.shape["tp"]

    def body(*args):
        return shards(cp_size, tp_size, *args)

    return jax.shard_map(body, mesh=mesh, in_specs=in_specs, out_specs=out_specs, check_vma=False)
```

profile of v0, /device:TPU:0, one launch (start us, length us, event | category | flops | bytes accessed | tf_op | source)
XLA Modules:
  0.0 47.3 jit_solution(89299688542247887)
XLA Ops:
  0.0 0.5 %collective-permute-start.1 = (bf16[512,8192]{1,0:T(8,128)(2,1)}, bf16[512,8192]{1,0:T(8,128)(2,1)}, u32[]{:S(2)}, u32[]{:S(2)}) collective-permute-start(bf16[512,8192]{1,0:T(8,128)(2,1)} %own_w_ref.3), channel_id=1, source_target_pairs={{0,1},{1,0},{2,3},{3,2},{4,5},{5,4},{6,7},{7,6},{8,9},{9,8},{10,11... | collective-permute-start | bytes 25165832 | tf_op jit(solution)/shard_map/ppermute | solution.py:131
  0.5 0.8 %constant_dynamic-slice_fusion = (bf16[192,128]{1,0:T(8,128)(2,1)S(1)}, bf16[192,128]{1,0:T(8,128)(2,1)S(1)}) fusion(bf16[192,256]{1,0:T(8,128)(2,1)} %param.7, s32[]{:T(128)S(6)} %select_n.136, bf16[192,256]{1,0:T(8,128)(2,1)} %param.6), kind=kLoop, calls=%fused_computation.4 | loop fusion | bytes 196612 | tf_op jit(solution)/shard_map/dynamic_slice | solution.py:138
  1.3 4.7 %collective-permute-start.2 = (bf16[192,256]{1,0:T(8,128)(2,1)S(1)}, bf16[192,256]{1,0:T(8,128)(2,1)S(1)}, u32[]{:S(2)}, u32[]{:S(2)}) collective-permute-start(bf16[192,256]{1,0:T(8,128)(2,1)S(1)} %pad_maximum_fusion.2.refs_5_), channel_id=1, source_target_pairs={{0,24},{1,17},{2,26},{3,19},{4,28},{5,21},{6,30},{7,23},{8,16},{9,... | collective-permute-start | bytes 294920 | tf_op jit(solution)/shard_map/ppermute | solution.py:131
  6.0 1.1 %collective-permute-start.3 = (bf16[192,256]{1,0:T(8,128)(2,1)S(1)}, bf16[192,256]{1,0:T(8,128)(2,1)S(1)}, u32[]{:S(2)}, u32[]{:S(2)}) collective-permute-start(bf16[192,256]{1,0:T(8,128)(2,1)S(1)} %pad_maximum_fusion.2.refs_5_), channel_id=1, source_target_pairs={{0,28},{1,21},{2,30},{3,23},{4,24},{5,17},{6,26},{7,19},{8,20},{9,... | collective-permute-start | bytes 294920 | tf_op jit(solution)/shard_map/ppermute | solution.py:131
  7.1 0.0 collective-permute-start.4
  7.1 0.9 %constant_dynamic-slice_fusion.3 = (bf16[48,512]{1,0:T(8,128)(2,1)S(1)}, bf16[48,512]{1,0:T(8,128)(2,1)S(1)}, bf16[48,512]{1,0:T(8,128)(2,1)S(1)}, bf16[48,512]{1,0:T(8,128)(2,1)S(1)}) fusion(bf16[192,512]{1,0:T(8,128)(2,1)} %param.5, s32[]{:T(128)S(6)} %select_n.133, s32[]{:T(128)S(6)} %select_n.130, s32[]{:T(128)S(6)} %select_n.126, s32[]{:T(128)S(6)} %select_n.134), kind=kLoop, calls=%fused_computation.7 | loop fusion | bytes 393232 | tf_op jit(solution)/shard_map/dynamic_slice | solution.py:157
  8.0 0.4 collective-permute-start
  8.5 1.1 %fusion.1 = (s32[192]{0:T(256)S(1)}, s32[192]{0:T(256)S(1)}, s32[192]{0:T(256)S(1)}, s32[192]{0:T(256)S(1)}, s32[192]{0:T(256)S(1)}, /*index=5*/s32[192]{0:T(256)S(1)}, s32[192]{0:T(256)S(1)}, s32[192]{0:T(256)S(1)}) fusion(s32[1536]{0:T(1024)} %param.8, s32[]{:T(128)S(6)} %select_n.123, s32[]{:T(128)S(6)} %select_n.121, s32[]{:T(128)S(6)} %select_n.119, ...), kind=kLoop, calls=%fused_computation.12 | loop fusion | bytes 12320 | tf_op jit(solution)/shard_map/dynamic_slice | solution.py:170
  9.5 0.1 concatenate.15
  9.6 0.8 %fusion = (s32[48]{0:T(128)S(1)}, s32[48]{0:T(128)S(1)}) fusion(s32[1536]{0:T(1024)} %param.8, s32[]{:T(128)S(6)} %dynamic_slice.61, s32[]{:T(128)S(6)} %dynamic_slice.63), kind=kLoop, calls=%fused_computation.11 | loop fusion | bytes 776 | tf_op jit(solution)/shard_map/dynamic_slice | solution.py:157
  10.5 0.1 pad_add_fusion
  10.5 0.1 compare_select_fusion.refs_0_
  10.6 3.0 %collective-permute-done.refs_2_ = bf16[96,512]{1,0:T(8,128)(2,1)S(1)} collective-permute-done((bf16[96,512]{1,0:T(8,128)(2,1)S(1)}, bf16[96,512]{1,0:T(8,128)(2,1)S(1)}, u32[]{:S(2)}, u32[]{:S(2)}) %collective-permute-start) | collective-permute-done | bytes 98336 | tf_op jit(solution)/shard_map/ppermute | solution.py:131
  13.6 2.8 %collective-permute-start.5 = (bf16[192,256]{1,0:T(8,128)(2,1)S(1)}, bf16[192,256]{1,0:T(8,128)(2,1)S(1)}, u32[]{:S(2)}, u32[]{:S(2)}) collective-permute-start(bf16[192,256]{1,0:T(8,128)(2,1)S(1)} %pad_maximum_fusion.2.refs_5_), channel_id=1, source_target_pairs={{0,4},{1,5},{2,6},{3,7},{4,0},{5,1},{6,2},{7,3},{8,12},{9,13},{10,... | collective-permute-start | bytes 294920 | tf_op jit(solution)/shard_map/ppermute | solution.py:131
  16.5 0.0 collective-permute-done.2.refs_6_
  16.5 0.0 collective-permute-start.6
  16.5 0.0 collective-permute-done.3.refs_7_
  16.5 0.5 %collective-permute-start.7 = (bf16[192,256]{1,0:T(8,128)(2,1)S(1)}, bf16[192,256]{1,0:T(8,128)(2,1)S(1)}, u32[]{:S(2)}, u32[]{:S(2)}) collective-permute-start(bf16[192,256]{1,0:T(8,128)(2,1)S(1)} %collective-permute-done.3.refs_7_), channel_id=1, source_target_pairs={{0,1},{1,0},{2,3},{3,2},{4,5},{5,4},{6,7},{7,6},{8,9},{9,8},{10,11... | collective-permute-start | bytes 294920 | tf_op jit(solution)/shard_map/ppermute | solution.py:131
  17.0 0.0 collective-permute-done.4.refs_8_
  17.0 0.1 collective-permute-start.8
  17.1 2.5 %collective-permute-done.5.refs_9_ = bf16[192,256]{1,0:T(8,128)(2,1)S(1)} collective-permute-done((bf16[192,256]{1,0:T(8,128)(2,1)S(1)}, bf16[192,256]{1,0:T(8,128)(2,1)S(1)}, u32[]{:S(2)}, u32[]{:S(2)}) %collective-permute-start.5) | collective-permute-done | bytes 98336 | tf_op jit(solution)/shard_map/ppermute | solution.py:131
  19.6 0.0 collective-permute-done.6.refs_10_
  19.6 0.0 collective-permute-done.7.refs_11_
  19.6 0.0 collective-permute-done.8.refs_12_
  19.6 0.0 collective-permute-done.1.refs_4_.sib_w_ref
  19.6 3.0 %attention.1 = (bf16[96,1024]{1,0:T(8,128)(2,1)S(1)}, bf16[48,2048]{1,0:T(8,128)(2,1)S(1)}, bf16[48,2048]{1,0:T(8,128)(2,1)S(1)}) custom-call(f32[96,1536]{1,0:T(8,128)S(1)} %compare_select_fusion.refs_0_, bf16[96,512]{1,0:T(8,128)(2,1)S(1)} %pad_maximum_fusion.refs_1_, bf16[96,512]{1,0:T(8,128)(2,1)S(1)} %collective-permute-done.refs_2_, ...), custom_call_target="tpu_custom_call" | custom-call | tf_op jit(solution)/shard_map/attention/pallas_call | solution.py:189
  22.7 3.2 %project.3 = (bf16[48,3072]{1,0:T(8,128)(2,1)S(1)}, bf16[48,3072]{1,0:T(8,128)(2,1)S(1)}) custom-call(bf16[96,1024]{1,0:T(8,128)(2,1)S(1)} %get-tuple-element.12.attended_ref, bf16[512,8192]{1,0:T(8,128)(2,1)} %own_w_ref.3, bf16[512,8192]{1,0:T(8,128)(2,1)} %collective-permute-done.1.refs_4_.sib_w_ref), custom_call_target="tpu_custom_call" | custom-call | tf_op jit(solution)/shard_map/project/pallas_call | solution.py:201
  25.9 1.8 %collective-permute-start.10 = (bf16[48,3072]{1,0:T(8,128)(2,1)S(1)}, bf16[48,3072]{1,0:T(8,128)(2,1)S(1)}, u32[]{:S(2)}, u32[]{:S(2)}) collective-permute-start(bf16[48,3072]{1,0:T(8,128)(2,1)S(1)} %get-tuple-element.16), channel_id=1, source_target_pairs={{0,2},{1,3},{2,0},{3,1},{4,6},{5,7},{6,4},{7,5},{8,10},{9,11},{10,... | collective-permute-start | bytes 884744 | tf_op jit(solution)/shard_map/ppermute | solution.py:131
  27.7 3.2 %project.2 = (bf16[48,3072]{1,0:T(8,128)(2,1)S(1)}, bf16[48,3072]{1,0:T(8,128)(2,1)S(1)}) custom-call(bf16[96,1024]{1,0:T(8,128)(2,1)S(1)} %get-tuple-element.12.attended_ref, bf16[512,8192]{1,0:T(8,128)(2,1)} %own_w_ref.3, bf16[512,8192]{1,0:T(8,128)(2,1)} %collective-permute-done.1.refs_4_.sib_w_ref), custom_call_target="tpu_custom_call" | custom-call | tf_op jit(solution)/shard_map/project/pallas_call | solution.py:201
  31.0 0.3 collective-permute-start.9
  31.3 1.8 %collective-permute-start.11 = (bf16[48,2048]{1,0:T(8,128)(2,1)S(1)}, bf16[48,2048]{1,0:T(8,128)(2,1)S(1)}, u32[]{:S(2)}, u32[]{:S(2)}) collective-permute-start(bf16[48,2048]{1,0:T(8,128)(2,1)S(1)} %get-tuple-element.18), channel_id=1, source_target_pairs={{0,2},{1,3},{2,0},{3,1},{4,6},{5,7},{6,4},{7,5},{8,10},{9,11},{10,... | collective-permute-start | bytes 589832 | tf_op jit(solution)/shard_map/ppermute | solution.py:131
  33.1 11.9 %collective-permute-done.11.refs_1_ = bf16[48,2048]{1,0:T(8,128)(2,1)S(1)} collective-permute-done((bf16[48,2048]{1,0:T(8,128)(2,1)S(1)}, bf16[48,2048]{1,0:T(8,128)(2,1)S(1)}, u32[]{:S(2)}, u32[]{:S(2)}) %collective-permute-start.11) | collective-permute-done | bytes 196640 | tf_op jit(solution)/shard_map/ppermute | solution.py:131
  45.0 0.7 %finish.3.refs_2_ = bf16[48,8192]{1,0:T(8,128)(2,1)} custom-call(bf16[48,2048]{1,0:T(8,128)(2,1)S(1)} %get-tuple-element.17.refs_0_, bf16[48,2048]{1,0:T(8,128)(2,1)S(1)} %collective-permute-done.11.refs_1_), custom_call_target="tpu_custom_call" | custom-call | tf_op jit(solution)/shard_map/finish/pallas_call | solution.py:216
  45.7 0.0 collective-permute-done.10.refs_1_
  45.7 0.8 %finish.4.refs_2_ = bf16[48,8192]{1,0:T(8,128)(2,1)} custom-call(bf16[48,3072]{1,0:T(8,128)(2,1)S(1)} %get-tuple-element.15.refs_0_, bf16[48,3072]{1,0:T(8,128)(2,1)S(1)} %collective-permute-done.10.refs_1_, bf16[48,8192]{1,0:T(8,128)(2,1)} %finish.3.refs_2_), custom_call_target="tpu_custom_call", output_to_operand_aliasing={{}: (2, {})} | custom-call | tf_op jit(solution)/shard_map/finish/pallas_call | solution.py:216
  46.5 0.0 collective-permute-done.9.refs_1_
  46.5 0.8 %finish.5 = bf16[48,8192]{1,0:T(8,128)(2,1)} custom-call(bf16[48,3072]{1,0:T(8,128)(2,1)S(1)} %get-tuple-element.13.refs_0_, bf16[48,3072]{1,0:T(8,128)(2,1)S(1)} %collective-permute-done.9.refs_1_, bf16[48,8192]{1,0:T(8,128)(2,1)} %finish.4.refs_2_), custom_call_target="tpu_custom_call", output_to_operand_aliasing={{}: (2, {})} | custom-call | tf_op jit(solution)/shard_map/finish/pallas_call | solution.py:216
  (3 shorter events, 0.0 us)
Async XLA Ops:
  0.0 19.6 %collective-permute-start.1 = (bf16[512,8192]{1,0:T(8,128)(2,1)}, bf16[512,8192]{1,0:T(8,128)(2,1)}, u32[]{:S(2)}, u32[]{:S(2)}) collective-permute-start(bf16[512,8192]{1,0:T(8,128)(2,1)} %own_w_ref.3), channel_id=1, source_target_pairs={{0,1},{1,0},{2,3},{3,2},{4,5},{5,4},{6,7},{7,6},{8,9},{9,8},{10,11... | collective-permute-start | bytes 25165832 | tf_op jit(solution)/shard_map/ppermute | solution.py:131
  1.3 15.1 %collective-permute-start.2 = (bf16[192,256]{1,0:T(8,128)(2,1)S(1)}, bf16[192,256]{1,0:T(8,128)(2,1)S(1)}, u32[]{:S(2)}, u32[]{:S(2)}) collective-permute-start(bf16[192,256]{1,0:T(8,128)(2,1)S(1)} %pad_maximum_fusion.2.refs_5_), channel_id=1, source_target_pairs={{0,24},{1,17},{2,26},{3,19},{4,28},{5,21},{6,30},{7,23},{8,16},{9,... | collective-permute-start | bytes 294920 | tf_op jit(solution)/shard_map/ppermute | solution.py:131
  6.0 10.5 %collective-permute-start.3 = (bf16[192,256]{1,0:T(8,128)(2,1)S(1)}, bf16[192,256]{1,0:T(8,128)(2,1)S(1)}, u32[]{:S(2)}, u32[]{:S(2)}) collective-permute-start(bf16[192,256]{1,0:T(8,128)(2,1)S(1)} %pad_maximum_fusion.2.refs_5_), channel_id=1, source_target_pairs={{0,28},{1,21},{2,30},{3,23},{4,24},{5,17},{6,26},{7,19},{8,20},{9,... | collective-permute-start | bytes 294920 | tf_op jit(solution)/shard_map/ppermute | solution.py:131
  7.1 9.9 %collective-permute-start.4 = (bf16[192,256]{1,0:T(8,128)(2,1)S(1)}, bf16[192,256]{1,0:T(8,128)(2,1)S(1)}, u32[]{:S(2)}, u32[]{:S(2)}) collective-permute-start(bf16[192,256]{1,0:T(8,128)(2,1)S(1)} %pad_maximum_fusion.2.refs_5_), channel_id=1, source_target_pairs={{0,8},{1,13},{2,10},{3,15},{4,12},{5,9},{6,14},{7,11},{8,0},{9,5},... | collective-permute-start | bytes 294920 | tf_op jit(solution)/shard_map/ppermute | solution.py:131
  8.0 5.6 %collective-permute-start = (bf16[96,512]{1,0:T(8,128)(2,1)S(1)}, bf16[96,512]{1,0:T(8,128)(2,1)S(1)}, u32[]{:S(2)}, u32[]{:S(2)}) collective-permute-start(bf16[96,512]{1,0:T(8,128)(2,1)S(1)} %pad_maximum_fusion.1), channel_id=1, source_target_pairs={{0,1},{1,0},{2,3},{3,2},{4,5},{5,4},{6,7},{7,6},{8,9},{9,8},{10,11... | collective-permute-start | bytes 294920 | tf_op jit(solution)/shard_map/ppermute | solution.py:131
  13.6 5.9 %collective-permute-start.5 = (bf16[192,256]{1,0:T(8,128)(2,1)S(1)}, bf16[192,256]{1,0:T(8,128)(2,1)S(1)}, u32[]{:S(2)}, u32[]{:S(2)}) collective-permute-start(bf16[192,256]{1,0:T(8,128)(2,1)S(1)} %pad_maximum_fusion.2.refs_5_), channel_id=1, source_target_pairs={{0,4},{1,5},{2,6},{3,7},{4,0},{5,1},{6,2},{7,3},{8,12},{9,13},{10,... | collective-permute-start | bytes 294920 | tf_op jit(solution)/shard_map/ppermute | solution.py:131
  16.5 3.1 %collective-permute-start.6 = (bf16[192,256]{1,0:T(8,128)(2,1)S(1)}, bf16[192,256]{1,0:T(8,128)(2,1)S(1)}, u32[]{:S(2)}, u32[]{:S(2)}) collective-permute-start(bf16[192,256]{1,0:T(8,128)(2,1)S(1)} %collective-permute-done.2.refs_6_), channel_id=1, source_target_pairs={{0,1},{1,0},{2,3},{3,2},{4,5},{5,4},{6,7},{7,6},{8,9},{9,8},{10,11... | collective-permute-start | bytes 294920 | tf_op jit(solution)/shard_map/ppermute | solution.py:131
  16.5 3.1 %collective-permute-start.7 = (bf16[192,256]{1,0:T(8,128)(2,1)S(1)}, bf16[192,256]{1,0:T(8,128)(2,1)S(1)}, u32[]{:S(2)}, u32[]{:S(2)}) collective-permute-start(bf16[192,256]{1,0:T(8,128)(2,1)S(1)} %collective-permute-done.3.refs_7_), channel_id=1, source_target_pairs={{0,1},{1,0},{2,3},{3,2},{4,5},{5,4},{6,7},{7,6},{8,9},{9,8},{10,11... | collective-permute-start | bytes 294920 | tf_op jit(solution)/shard_map/ppermute | solution.py:131
  17.0 2.6 %collective-permute-start.8 = (bf16[192,256]{1,0:T(8,128)(2,1)S(1)}, bf16[192,256]{1,0:T(8,128)(2,1)S(1)}, u32[]{:S(2)}, u32[]{:S(2)}) collective-permute-start(bf16[192,256]{1,0:T(8,128)(2,1)S(1)} %collective-permute-done.4.refs_8_), channel_id=1, source_target_pairs={{0,1},{1,0},{2,3},{3,2},{4,5},{5,4},{6,7},{7,6},{8,9},{9,8},{10,11... | collective-permute-start | bytes 294920 | tf_op jit(solution)/shard_map/ppermute | solution.py:131
  25.9 19.8 %collective-permute-start.10 = (bf16[48,3072]{1,0:T(8,128)(2,1)S(1)}, bf16[48,3072]{1,0:T(8,128)(2,1)S(1)}, u32[]{:S(2)}, u32[]{:S(2)}) collective-permute-start(bf16[48,3072]{1,0:T(8,128)(2,1)S(1)} %get-tuple-element.16), channel_id=1, source_target_pairs={{0,2},{1,3},{2,0},{3,1},{4,6},{5,7},{6,4},{7,5},{8,10},{9,11},{10,... | collective-permute-start | bytes 884744 | tf_op jit(solution)/shard_map/ppermute | solution.py:131
  31.0 15.6 %collective-permute-start.9 = (bf16[48,3072]{1,0:T(8,128)(2,1)S(1)}, bf16[48,3072]{1,0:T(8,128)(2,1)S(1)}, u32[]{:S(2)}, u32[]{:S(2)}) collective-permute-start(bf16[48,3072]{1,0:T(8,128)(2,1)S(1)} %get-tuple-element.14), channel_id=1, source_target_pairs={{0,2},{1,3},{2,0},{3,1},{4,6},{5,7},{6,4},{7,5},{8,10},{9,11},{10,... | collective-permute-start | bytes 884744 | tf_op jit(solution)/shard_map/ppermute | solution.py:131
  31.3 13.7 %collective-permute-start.11 = (bf16[48,2048]{1,0:T(8,128)(2,1)S(1)}, bf16[48,2048]{1,0:T(8,128)(2,1)S(1)}, u32[]{:S(2)}, u32[]{:S(2)}) collective-permute-start(bf16[48,2048]{1,0:T(8,128)(2,1)S(1)} %get-tuple-element.18), channel_id=1, source_target_pairs={{0,2},{1,3},{2,0},{3,1},{4,6},{5,7},{6,4},{7,5},{8,10},{9,11},{10,... | collective-permute-start | bytes 589832 | tf_op jit(solution)/shard_map/ppermute | solution.py:131
where the time goes:
time: 47.7 us; the launch traced here: 47.3 us
  waiting for transfers between devices  17.4 us (36%)
  starting transfers between devices  14.1 us (30%)
  Pallas kernels  11.8 us (25%)
  local copies, waits for them, and re-layouts  3.71 us (8%)
    ppermute x12, waiting for transfers between devices, permute(): return lax.ppermute(x, AXES, pairs)  17.4 us
    ppermute x12, starting transfers between devices, permute(): return lax.ppermute(x, AXES, pairs)  14.1 us
    pallas_call x2, Pallas kernels, shards(): pl.pallas_call(functools.partial(project_kernel, lo), in_specs=[whole, hb...  6.46 us
    pallas_call x1, Pallas kernels, shards(): pl.pallas_call(functools.partial(attention_kernel, stack), in_specs=[whol...  3.05 us
    pallas_call x3, Pallas kernels, shards(): pl.pallas_call(functools.partial(finish_kernel, lo), in_specs=[whole, who...  2.32 us
    dynamic_slice x2, local copies, waits for them, and re-layouts, rows_of(): lax.dynamic_slice_in_dim(x, ((tp // 2 + s) % 2 * 2 + c) * part, part, 0)  1.73 us
    dynamic_slice x1, local copies, waits for them, and re-layouts, shards(): lax.dynamic_slice_in_dim(positions, (cp ^ jnp.where(core == 0, a, b)) * r...  1.07 us
  transfers between devices with their start and end apart: 12, of which 3 were waited for; matrix products, arithmetic and copies ran while one was open for 8% of the time, Pallas kernels for 10%

commit v1 on v0

v1 whole, which is shorter than its diff:
```python
import functools

import jax
import jax.numpy as jnp
from jax import lax
from jax.experimental import pallas as pl
from jax.experimental.pallas import tpu as pltpu
from jax.sharding import PartitionSpec as P


HEAD = 128
GROUP = 8
NEG = -1e30
LOG2E = 1.4426950408889634
AXES = ("cp", "tp")
VMEM_LIMIT = 36 * 2**20
COLUMN_CUTS = (0, 2, 6, 11, 16)
TILE = 512


def attend(stack, bias_ref, own_ref, sib_ref, first_row, block_refs, out_ref):
    keys = jnp.concatenate([r[:, :HEAD] for r in block_refs], axis=0)
    values = jnp.concatenate([r[:, HEAD:] for r in block_refs], axis=0)
    values = jnp.concatenate([values, jnp.ones_like(values)], axis=1)
    scale = HEAD ** (-0.5) * LOG2E
    rows = out_ref.shape[0]
    heads = own_ref.shape[1] // HEAD
    at_rows = slice(first_row, first_row + rows)
    for side, q_ref in enumerate((own_ref, sib_ref)):
        for first in range(0, heads, stack):
            q = jnp.concatenate(
                [q_ref[at_rows, h * HEAD : (h + 1) * HEAD] for h in range(first, first + stack)],
                axis=0,
            )
            scores = lax.dot_general(
                q, keys, (((1,), (1,)), ((), ())), preferred_element_type=jnp.float32
            )
            mask = bias_ref[at_rows, :][None]
            scores = (scores.reshape(stack, rows, -1) + mask).reshape(scores.shape)
            top = jnp.max(scores, axis=1, keepdims=True)
            weights = jnp.exp2((scores - top) * scale).astype(jnp.bfloat16)
            mixed = jnp.dot(weights, values, preferred_element_type=jnp.float32)
            result = (mixed[:, :HEAD] / mixed[:, HEAD:]).astype(jnp.bfloat16)
            for i in range(stack):
                at = (side * heads + first + i) * HEAD
                out_ref[:, at : at + HEAD] = result[i * rows : (i + 1) * rows]


def weight_loads(first, own_w_ref, sib_w_ref, weight_ref, sems):
    half = own_w_ref.shape[0]
    tiles, _, tile = weight_ref.shape
    return [
        [
            pltpu.make_async_copy(
                ref.at[:, pl.ds(first + t * tile, tile)],
                weight_ref.at[t, pl.ds(i * half, half)],
                sems.at[t, i],
            )
            for i, ref in enumerate((own_w_ref, sib_w_ref))
        ]
        for t in range(tiles)
    ]


def project(first, attended_refs, weight_refs, out_refs, weight_ref, sems, beside=None):
    loads = weight_loads(first, *weight_refs, weight_ref, sems)
    for pair in loads:
        for load in pair:
            load.start()
    if beside:
        beside()
    tile = weight_ref.shape[2]
    for t, pair in enumerate(loads):
        for load in pair:
            load.wait()
        rows = jnp.concatenate([r[...] for r in attended_refs], axis=0)
        partial = jnp.dot(rows, weight_ref[t], preferred_element_type=jnp.float32)
        partial = partial.astype(jnp.bfloat16)
        at = 0
        for ref in out_refs:
            ref[:, pl.ds(t * tile, tile)] = partial[at : at + ref.shape[0]]
            at += ref.shape[0]


def prepare_kernel(offsets, positions_ref, queries_ref, own_w_ref, *refs):
    bias_ref, own_ref, swap_ref, weight_ref, sems = refs
    rows = queries_ref.shape[0]
    part = own_ref.shape[0] // 2
    run = rows // 2
    cp, tp = lax.axis_index("cp"), lax.axis_index("tp")
    side, core = tp // 2, tp % 2
    loads = [
        pltpu.make_async_copy(
            own_w_ref.at[:, pl.ds(0, weight_ref.shape[1])], weight_ref, sems.at[0]
        )
    ]
    for i, ref in enumerate((own_ref, swap_ref)):
        for half in range(2):
            row = ((side + half) % 2 * 2 + (core + i) % 2) * part
            loads.append(
                pltpu.make_async_copy(
                    queries_ref.at[pl.ds(row, part)],
                    ref.at[pl.ds(half * part, part)],
                    sems.at[1 + 2 * i + half],
                )
            )
    for load in loads[1:] + loads[:1]:
        load.start()
    lane = lax.broadcasted_iota(jnp.int32, (1, bias_ref.shape[1]), 1)
    key_pos = lane
    for j, (a, b) in enumerate(offsets):
        block = cp ^ jnp.where(core == 0, a, b)
        for half in range(2):
            at = j * rows + half * run
            start = positions_ref[block * rows + half * run]
            key_pos = jnp.where(lane >= at, lane + (start - at), key_pos)
    step = lax.broadcasted_iota(jnp.int32, (part, 1), 0)
    for half in range(2):
        token = ((side + half) % 2 * 2 + core) * part
        query_pos = positions_ref[cp * rows + token] + step
        bias_ref[pl.ds(half * part, part), :] = jnp.where(
            key_pos <= query_pos, 0.0, NEG
        ).astype(jnp.float32)
    for load in loads:
        load.wait()


def send_kernel(stack, bias_ref, own_ref, sib_ref, own_part_ref, sib_w_ref, *refs):
    block_refs = refs[:-4]
    attended_ref, out_ref, sib_part_ref, sems = refs[-4:]
    width = out_ref.shape[1]
    total = sib_part_ref.shape[1]
    loads = [
        pltpu.make_async_copy(sib_w_ref.at[:, cols], sib_part_ref.at[:, cols], sems.at[i])
        for i, cols in enumerate((pl.ds(0, width), pl.ds(width, total - width)))
    ]
    for load in loads:
        load.start()

    @pl.when(bias_ref[0, 0] <= 0.0)
    def _():
        row = attended_ref.shape[0]
        attend(stack, bias_ref, own_ref, sib_ref, row, block_refs, attended_ref)

    loads[0].wait()
    resident(pl.ds(0, width), attended_ref, own_part_ref, sib_part_ref, out_ref)
    loads[1].wait()


def resident(cols, attended_ref, own_part_ref, sib_part_ref, out_ref):
    half = own_part_ref.shape[0]
    partial = jnp.dot(
        attended_ref[:, :half], own_part_ref[:, cols], preferred_element_type=jnp.float32
    ) + jnp.dot(attended_ref[:, half:], sib_part_ref[:, cols], preferred_element_type=jnp.float32)
    out_ref[...] = partial.astype(jnp.bfloat16)


def resident_kernel(first, attended_ref, own_part_ref, sib_part_ref, *out_refs):
    for ref in out_refs:
        cols = pl.ds(first, ref.shape[1])
        resident(cols, attended_ref, own_part_ref, sib_part_ref, ref)
        first += ref.shape[1]


def keep_kernel(stack, first, bias_ref, own_ref, sib_ref, own_w_ref, sib_w_ref, sent_ref, *refs):
    block_refs = refs[:-5]
    attended_ref, keep_ref, send_ref, weight_ref, sems = refs[-5:]

    def attention():
        @pl.when(bias_ref[0, 0] <= 0.0)
        def _():
            attend(stack, bias_ref, own_ref, sib_ref, 0, block_refs, attended_ref)

    project(
        first,
        (attended_ref, sent_ref),
        (own_w_ref, sib_w_ref),
        (keep_ref, send_ref),
        weight_ref,
        sems,
        attention,
    )


def project_kernel(first, own_w_ref, sib_w_ref, *refs):
    count = (len(refs) - 2) // 2
    project(
        first, refs[:count], (own_w_ref, sib_w_ref), refs[count:-2], refs[-2], refs[-1]
    )


def finish_kernel(first, *refs):
    keep_ref, got_ref = refs[:2]
    out_ref, sum_ref, sem = refs[-3:]
    sum_ref[...] = (
        keep_ref[...].astype(jnp.float32) + got_ref[...].astype(jnp.float32)
    ).astype(jnp.bfloat16)
    store = pltpu.make_async_copy(
        sum_ref, out_ref.at[:, pl.ds(first, sum_ref.shape[1])], sem
    )
    store.start()
    store.wait()


def pairing(cp_size):
    return [(o, o + 1) for o in range(cp_size - 2, 0, -2)]


def shards(cp_size, tp_size, queries, keys, values, positions, out_weight):
    rows = queries.shape[0]
    heads = queries.shape[1] // HEAD
    part = rows // tp_size
    tp = lax.axis_index("tp")

    def permute(x, to_cp, to_tp):
        pairs = [
            (c * tp_size + t, to_cp(c, t) * tp_size + to_tp(t))
            for c in range(cp_size)
            for t in range(tp_size)
        ]
        return lax.ppermute(x, AXES, pairs)

    def to_sibling(x):
        return permute(x, lambda c, t: c, lambda t: t ^ 1)

    kv_group = tp * heads // GROUP
    block = jnp.concatenate(
        [lax.dynamic_slice_in_dim(a, kv_group * HEAD, HEAD, 1) for a in (keys, values)], axis=1
    )
    blocks = [block]
    offsets = [(0, 0)]
    fetched = []
    for pair in pairing(cp_size):
        arrived = permute(block, lambda c, t, pair=pair: c ^ pair[t & 1], lambda t: t)
        fetched.append(arrived)
        blocks.append(arrived)
        offsets.append(pair)
    blocks.append(permute(block, lambda c, t: c ^ 1, lambda t: t))
    offsets.append((1, 1))
    for arrived, pair in zip(fetched, pairing(cp_size)):
        blocks.append(to_sibling(arrived))
        offsets.append((pair[1], pair[0]))

    width = out_weight.shape[1]
    cuts = [c * width // COLUMN_CUTS[-1] for c in COLUMN_CUTS]
    vmem = functools.partial(pltpu.with_memory_space_constraint, memory_space=pltpu.VMEM)
    sib_weight = to_sibling(out_weight)
    hbm = pl.BlockSpec(memory_space=pltpu.HBM)
    weights = [pltpu.with_memory_space_constraint(w, pltpu.HBM) for w in (out_weight, sib_weight)]
    whole = pl.BlockSpec(memory_space=pltpu.VMEM)
    token_count = positions.shape[0]
    stack = min(heads, max(1, 4 * 1536 // token_count))
    depth = 2 * heads * HEAD
    attended = pltpu.VMEM((part, depth), jnp.bfloat16)
    mine = (2 * part, heads * HEAD)
    bias, own_q, swap_q, own_part = pl.pallas_call(
        functools.partial(prepare_kernel, offsets),
        in_specs=[pl.BlockSpec(memory_space=pltpu.SMEM), hbm, hbm],
        out_shape=(
            pltpu.VMEM((2 * part, token_count), jnp.float32),
            pltpu.VMEM(mine, jnp.bfloat16),
            pltpu.VMEM(mine, jnp.bfloat16),
            pltpu.VMEM((heads * HEAD, cuts[2]), jnp.bfloat16),
        ),
        scratch_shapes=[pltpu.SemaphoreType.DMA((5,))],
        compiler_params=pltpu.CompilerParams(vmem_limit_bytes=VMEM_LIMIT),
        name="prepare",
    )(positions, pltpu.with_memory_space_constraint(queries, pltpu.HBM), weights[0])
    sib_q = to_sibling(swap_q)
    inputs = [vmem(bias), vmem(own_q), vmem(sib_q)]
    kv = [vmem(b) for b in blocks]

    def call(kernel, lo, hi, operands, in_specs, out_shape):
        return pl.pallas_call(
            kernel,
            in_specs=in_specs,
            out_shape=out_shape,
            scratch_shapes=[
                pltpu.VMEM(((hi - lo) // TILE, depth, TILE), jnp.bfloat16),
                pltpu.SemaphoreType.DMA(((hi - lo) // TILE, 2)),
            ],
            compiler_params=pltpu.CompilerParams(vmem_limit_bytes=VMEM_LIMIT),
        )(*operands)

    spans = list(zip(cuts[:-1], cuts[1:]))
    kept = [None] * len(spans)
    got = []
    for n, (lo, hi) in enumerate(spans):
        half = pltpu.VMEM((part, hi - lo), jnp.bfloat16)
        if n == 0:
            parts = pltpu.VMEM((depth // 2, cuts[2]), jnp.bfloat16)
            sent_rows, send, sib_part = pl.pallas_call(
                functools.partial(send_kernel, stack),
                in_specs=[whole] * 4 + [hbm] + [whole] * len(kv),
                out_shape=(attended, half, parts),
                scratch_shapes=[pltpu.SemaphoreType.DMA((2,))],
                compiler_params=pltpu.CompilerParams(vmem_limit_bytes=VMEM_LIMIT),
                name="send",
            )(*inputs, vmem(own_part), weights[1], *kv)
            parts = [vmem(own_part), vmem(sib_part)]
        elif n == 1:
            send = pl.pallas_call(
                functools.partial(resident_kernel, lo),
                in_specs=[whole] * 3,
                out_shape=half,
                compiler_params=pltpu.CompilerParams(vmem_limit_bytes=VMEM_LIMIT),
                name="again",
            )(vmem(sent_rows), *parts)
        elif n == 2:
            kept_rows, kept[n], send = call(
                functools.partial(keep_kernel, stack, lo),
                lo,
                hi,
                [*inputs, *weights, sent_rows, *kv],
                [whole] * 3 + [hbm] * 2 + [whole] * (1 + len(kv)),
                (attended, half, half),
            )
        else:
            kept[n], send = call(
                functools.partial(project_kernel, lo),
                lo,
                hi,
                [*weights, kept_rows, sent_rows],
                [hbm] * 2 + [whole] * 2,
                (half, half),
            )
        got.append(permute(send, lambda c, t: c, lambda t: t ^ 2))
    kept[:2] = pl.pallas_call(
        functools.partial(resident_kernel, 0),
        in_specs=[whole] * 3,
        out_shape=[pltpu.VMEM((part, hi - lo), jnp.bfloat16) for lo, hi in spans[:2]],
        compiler_params=pltpu.CompilerParams(vmem_limit_bytes=VMEM_LIMIT),
        name="rest",
    )(vmem(kept_rows), *parts)
    out = ()
    for lo, hi, keep, arrived in zip(cuts[:-1], cuts[1:], kept, got):
        out = pl.pallas_call(
            functools.partial(finish_kernel, lo),
            in_specs=[whole, whole] + [hbm] * len(out),
            out_specs=(hbm,),
            out_shape=(pltpu.HBM((part, width), jnp.bfloat16),),
            scratch_shapes=[pltpu.VMEM((part, hi - lo), jnp.bfloat16), pltpu.SemaphoreType.DMA],
            input_output_aliases={2: 0} if out else {},
            name="finish",
        )(vmem(keep), vmem(arrived), *out)
    return out[0]


def solution(mesh):
    in_specs = (P("cp", "tp"), P("cp", None), P("cp", None), P(), P("tp", None))
    out_specs = P(("cp", "tp"), None)
    cp_size, tp_size = mesh.shape["cp"], mesh.shape["tp"]

    def body(*args):
        return shards(cp_size, tp_size, *args)

    return jax.shard_map(body, mesh=mesh, in_specs=in_specs, out_specs=out_specs, check_vma=False)
```

time: 47.7 us -> 45.8 us (0.960)
  Pallas kernels: 11.8 us -> 15.5 us
  local copies, waits for them, and re-layouts: 3.71 us -> 1.53 us
  waiting for transfers between devices: 17.4 us -> 15.6 us
  starting transfers between devices: 14.1 us -> 12.8 us
    pallas_call x3 -> x6, Pallas kernels: 9.5 us -> 12.5 us  [the longest x2 5.88 us: call(): pl.pallas_call(kernel, in_specs=in_specs, out_shape=out_shape, scratch_sh...]
    dynamic_slice x3 -> x0, local copies, waits for them, and re-layouts: 2.8 us -> none  [the longest x2 1.73 us: rows_of(): lax.dynamic_slice_in_dim(x, ((tp // 2 + s) % 2 * 2 + c) * part, part, 0)]
    ppermute x12 -> x13, waiting for transfers between devices: 17.4 us -> 15.6 us  [permute(): return lax.ppermute(x, AXES, pairs)]
    ppermute x12 -> x13, starting transfers between devices: 14.1 us -> 12.8 us  [permute(): return lax.ppermute(x, AXES, pairs)]
    unnamed x0 -> x2, local copies, waits for them, and re-layouts: none -> 0.7 us
    pallas_call x3 -> x4, Pallas kernels: 2.32 us -> 2.94 us  [shards(): pl.pallas_call(functools.partial(finish_kernel, lo), in_specs=[whole, who...]
  transfers between devices with their start and end apart: 12 -> 13, of which waited for: 3 -> 4; matrix products, arithmetic and copies ran while one was open for 8% -> 2% of each run, Pallas kernels for 10% -> 21%
where the time goes in v1:
time: 45.8 us; the launch traced here: 45.5 us
  waiting for transfers between devices  15.6 us (34%)
  Pallas kernels  15.5 us (34%)
  starting transfers between devices  12.8 us (28%)
  local copies, waits for them, and re-layouts  1.53 us (3%)
    ppermute x13, waiting for transfers between devices, permute(): return lax.ppermute(x, AXES, pairs)  15.6 us
    ppermute x13, starting transfers between devices, permute(): return lax.ppermute(x, AXES, pairs)  12.8 us
    pallas_call x2, Pallas kernels, call(): pl.pallas_call(kernel, in_specs=in_specs, out_shape=out_shape, scratch_sh...  5.88 us
    pallas_call x4, Pallas kernels, shards(): pl.pallas_call(functools.partial(finish_kernel, lo), in_specs=[whole, who...  2.94 us
    pallas_call x1, Pallas kernels, shards(): pl.pallas_call(functools.partial(prepare_kernel, offsets), in_specs=[pl.B...  2.71 us
    pallas_call x1, Pallas kernels, shards(): pl.pallas_call(functools.partial(send_kernel, stack), in_specs=[whole] *...  1.94 us
    pallas_call x1, Pallas kernels, shards(): pl.pallas_call(functools.partial(resident_kernel, 0), in_specs=[whole] *...  1.18 us
  transfers between devices with their start and end apart: 13, of which 4 were waited for; matrix products, arithmetic and copies ran while one was open for 2% of the time, Pallas kernels for 21%

profile of v1, /device:TPU:0, one launch (start us, length us, event | category | flops | bytes accessed | tf_op | source)
XLA Modules:
  0.0 45.5 jit_solution(8727351863373537285)
XLA Ops:
  0.0 0.5 %collective-permute-start = (bf16[512,8192]{1,0:T(8,128)(2,1)}, bf16[512,8192]{1,0:T(8,128)(2,1)}, u32[]{:S(2)}, u32[]{:S(2)}) collective-permute-start(bf16[512,8192]{1,0:T(8,128)(2,1)} %own_w_ref.5), channel_id=1, source_target_pairs={{0,1},{1,0},{2,3},{3,2},{4,5},{5,4},{6,7},{7,6},{8,9},{9,8},{10,11... | collective-permute-start | bytes 25165832 | tf_op jit(solution)/shard_map/ppermute | solution.py:221
  0.5 0.8 %constant_dynamic-slice_fusion = (bf16[192,128]{1,0:T(8,128)(2,1)S(1)}, bf16[192,128]{1,0:T(8,128)(2,1)S(1)}) fusion(bf16[192,256]{1,0:T(8,128)(2,1)} %param.7, s32[]{:T(128)S(6)} %select_n.10, bf16[192,256]{1,0:T(8,128)(2,1)} %param.6), kind=kLoop, calls=%fused_computation.1 | loop fusion | bytes 196612 | tf_op jit(solution)/shard_map/dynamic_slice | solution.py:228
  1.3 2.5 %collective-permute-start.5 = (bf16[192,256]{1,0:T(8,128)(2,1)S(1)}, bf16[192,256]{1,0:T(8,128)(2,1)S(1)}, u32[]{:S(2)}, u32[]{:S(2)}) collective-permute-start(bf16[192,256]{1,0:T(8,128)(2,1)S(1)} %pad_maximum_fusion.refs_0_), channel_id=1, source_target_pairs={{0,4},{1,5},{2,6},{3,7},{4,0},{5,1},{6,2},{7,3},{8,12},{9,13},{10,... | collective-permute-start | bytes 294920 | tf_op jit(solution)/shard_map/ppermute | solution.py:221
  3.9 1.6 %collective-permute-start.4 = (bf16[192,256]{1,0:T(8,128)(2,1)S(1)}, bf16[192,256]{1,0:T(8,128)(2,1)S(1)}, u32[]{:S(2)}, u32[]{:S(2)}) collective-permute-start(bf16[192,256]{1,0:T(8,128)(2,1)S(1)} %pad_maximum_fusion.refs_0_), channel_id=1, source_target_pairs={{0,8},{1,13},{2,10},{3,15},{4,12},{5,9},{6,14},{7,11},{8,0},{9,5},... | collective-permute-start | bytes 294920 | tf_op jit(solution)/shard_map/ppermute | solution.py:221
  5.5 2.6 %collective-permute-start.3 = (bf16[192,256]{1,0:T(8,128)(2,1)S(1)}, bf16[192,256]{1,0:T(8,128)(2,1)S(1)}, u32[]{:S(2)}, u32[]{:S(2)}) collective-permute-start(bf16[192,256]{1,0:T(8,128)(2,1)S(1)} %pad_maximum_fusion.refs_0_), channel_id=1, source_target_pairs={{0,16},{1,21},{2,18},{3,23},{4,20},{5,17},{6,22},{7,19},{8,24},{9,... | collective-permute-start | bytes 294920 | tf_op jit(solution)/shard_map/ppermute | solution.py:221
  8.0 0.2 collective-permute-start.2
  8.3 0.0 copy-start
  8.3 0.7 %copy-done = s32[1536]{0:T(1024)S(1)} copy-done((s32[1536]{0:T(1024)S(1)}, s32[1536]{0:T(1024)}, u32[]{:S(2)}) %copy-start) | copy-done | bytes 6168
  9.0 2.7 %prepare.1 = (f32[96,1536]{1,0:T(8,128)S(1)}, bf16[96,512]{1,0:T(8,128)(2,1)S(1)}, bf16[96,512]{1,0:T(8,128)(2,1)S(1)}, bf16[512,3072]{1,0:T(8,128)(2,1)S(1)}) custom-call(s32[1536]{0:T(1024)S(1)} %copy-done, bf16[192,512]{1,0:T(8,128)(2,1)} %queries_ref.1, bf16[512,8192]{1,0:T(8,128)(2,1)} %own_w_ref.5), custom_call_target="tpu_custom_call" | custom-call | tf_op jit(solution)/shard_map/prepare/pallas_call | solution.py:256
  11.7 0.0 collective-permute-done.5.refs_4_
  11.7 0.4 collective-permute-start.1
  12.1 0.0 collective-permute-done.4.refs_3_
  12.1 0.2 collective-permute-start.8
  12.3 4.0 %collective-permute-done.3.refs_2_ = bf16[192,256]{1,0:T(8,128)(2,1)S(1)} collective-permute-done((bf16[192,256]{1,0:T(8,128)(2,1)S(1)}, bf16[192,256]{1,0:T(8,128)(2,1)S(1)}, u32[]{:S(2)}, u32[]{:S(2)}) %collective-permute-start.3) | collective-permute-done | bytes 98336 | tf_op jit(solution)/shard_map/ppermute | solution.py:221
  16.2 0.0 collective-permute-start.7
  16.2 0.0 collective-permute-done.2.refs_1_
  16.2 0.5 %collective-permute-start.6 = (bf16[192,256]{1,0:T(8,128)(2,1)S(1)}, bf16[192,256]{1,0:T(8,128)(2,1)S(1)}, u32[]{:S(2)}, u32[]{:S(2)}) collective-permute-start(bf16[192,256]{1,0:T(8,128)(2,1)S(1)} %collective-permute-done.2.refs_1_), channel_id=1, source_target_pairs={{0,1},{1,0},{2,3},{3,2},{4,5},{5,4},{6,7},{7,6},{8,9},{9,8},{10,11... | collective-permute-start | bytes 294920 | tf_op jit(solution)/shard_map/ppermute | solution.py:221
  16.8 0.0 collective-permute-done.1.sib_ref
  16.8 0.0 collective-permute-done.8.refs_7_
  16.8 0.8 %collective-permute-done.7.refs_6_ = bf16[192,256]{1,0:T(8,128)(2,1)S(1)} collective-permute-done((bf16[192,256]{1,0:T(8,128)(2,1)S(1)}, bf16[192,256]{1,0:T(8,128)(2,1)S(1)}, u32[]{:S(2)}, u32[]{:S(2)}) %collective-permute-start.7) | collective-permute-done | bytes 98336 | tf_op jit(solution)/shard_map/ppermute | solution.py:221
  17.5 0.2 collective-permute-done.6.refs_5_
  17.7 0.0 collective-permute-done.sib_w_ref
  17.7 1.9 %send.1 = (bf16[48,1024]{1,0:T(8,128)(2,1)S(1)}, bf16[48,1024]{1,0:T(8,128)(2,1)S(1)}, bf16[512,3072]{1,0:T(8,128)(2,1)S(1)}) custom-call(f32[96,1536]{1,0:T(8,128)S(1)} %get-tuple-element.19.bias_ref, bf16[96,512]{1,0:T(8,128)(2,1)S(1)} %get-tuple-element.20.own_ref, bf16[96,512]{1,0:T(8,128)(2,1)S(1)} %collective-permute-done.1.sib_ref, ...), custom_call_target="tpu_custom_call" | custom-call | tf_op jit(solution)/shard_map/send/pallas_call | solution.py:292
  19.6 3.0 %shard_map.55 = (bf16[48,1024]{1,0:T(8,128)(2,1)S(1)}, bf16[48,2560]{1,0:T(8,128)(2,1)S(1)}, bf16[48,2560]{1,0:T(8,128)(2,1)S(1)}) custom-call(f32[96,1536]{1,0:T(8,128)S(1)} %get-tuple-element.19.bias_ref, bf16[96,512]{1,0:T(8,128)(2,1)S(1)} %get-tuple-element.20.own_ref, bf16[96,512]{1,0:T(8,128)(2,1)S(1)} %collective-permute-done.1.sib_ref, ...), custom_call_target="tpu_custom_call" | custom-call | tf_op jit(solution)/shard_map/pallas_call | solution.py:274
  22.6 1.6 %collective-permute-start.10 = (bf16[48,2560]{1,0:T(8,128)(2,1)S(1)}, bf16[48,2560]{1,0:T(8,128)(2,1)S(1)}, u32[]{:S(2)}, u32[]{:S(2)}) collective-permute-start(bf16[48,2560]{1,0:T(8,128)(2,1)S(1)} %get-tuple-element.28), channel_id=1, source_target_pairs={{0,2},{1,3},{2,0},{3,1},{4,6},{5,7},{6,4},{7,5},{8,10},{9,11},{10,... | collective-permute-start | bytes 737288 | tf_op jit(solution)/shard_map/ppermute | solution.py:221
  24.2 2.9 %shard_map.56 = (bf16[48,2560]{1,0:T(8,128)(2,1)S(1)}, bf16[48,2560]{1,0:T(8,128)(2,1)S(1)}) custom-call(bf16[512,8192]{1,0:T(8,128)(2,1)} %own_w_ref.5, bf16[512,8192]{1,0:T(8,128)(2,1)} %collective-permute-done.sib_w_ref, bf16[48,1024]{1,0:T(8,128)(2,1)S(1)} %get-tuple-element.24.refs_0_.attended_ref, ...), custom_call_target="tpu_custom_call" | custom-call | tf_op jit(solution)/shard_map/pallas_call | solution.py:274
  27.1 0.6 %collective-permute-start.9 = (bf16[48,2560]{1,0:T(8,128)(2,1)S(1)}, bf16[48,2560]{1,0:T(8,128)(2,1)S(1)}, u32[]{:S(2)}, u32[]{:S(2)}) collective-permute-start(bf16[48,2560]{1,0:T(8,128)(2,1)S(1)} %get-tuple-element.26), channel_id=1, source_target_pairs={{0,2},{1,3},{2,0},{3,1},{4,6},{5,7},{6,4},{7,5},{8,10},{9,11},{10,... | collective-permute-start | bytes 737288 | tf_op jit(solution)/shard_map/ppermute | solution.py:221
  27.7 0.8 %again.1 = bf16[48,2048]{1,0:T(8,128)(2,1)S(1)} custom-call(bf16[48,1024]{1,0:T(8,128)(2,1)S(1)} %get-tuple-element.23.sent_ref.refs_1_.attended_ref, bf16[512,3072]{1,0:T(8,128)(2,1)S(1)} %get-tuple-element.22.own_part_ref, bf16[512,3072]{1,0:T(8,128)(2,1)S(1)} %get-tuple-element.29.sib_part_ref), custom_call_target="tpu_custom_call" | custom-call | tf_op jit(solution)/shard_map/again/pallas_call | solution.py:302
  28.5 1.6 %collective-permute-start.11 = (bf16[48,2048]{1,0:T(8,128)(2,1)S(1)}, bf16[48,2048]{1,0:T(8,128)(2,1)S(1)}, u32[]{:S(2)}, u32[]{:S(2)}) collective-permute-start(bf16[48,2048]{1,0:T(8,128)(2,1)S(1)} %again.1), channel_id=1, source_target_pairs={{0,2},{1,3},{2,0},{3,1},{4,6},{5,7},{6,4},{7,5},{8,10},{9,11},{10,... | collective-permute-start | bytes 589832 | tf_op jit(solution)/shard_map/ppermute | solution.py:221
  30.1 0.5 %collective-permute-start.12 = (bf16[48,1024]{1,0:T(8,128)(2,1)S(1)}, bf16[48,1024]{1,0:T(8,128)(2,1)S(1)}, u32[]{:S(2)}, u32[]{:S(2)}) collective-permute-start(bf16[48,1024]{1,0:T(8,128)(2,1)S(1)} %get-tuple-element.32), channel_id=1, source_target_pairs={{0,2},{1,3},{2,0},{3,1},{4,6},{5,7},{6,4},{7,5},{8,10},{9,11},{10,... | collective-permute-start | bytes 294920 | tf_op jit(solution)/shard_map/ppermute | solution.py:221
  30.6 1.2 %rest.1 = (bf16[48,1024]{1,0:T(8,128)(2,1)S(1)}, bf16[48,2048]{1,0:T(8,128)(2,1)S(1)}) custom-call(bf16[48,1024]{1,0:T(8,128)(2,1)S(1)} %get-tuple-element.24.refs_0_.attended_ref, bf16[512,3072]{1,0:T(8,128)(2,1)S(1)} %get-tuple-element.22.own_part_ref, bf16[512,3072]{1,0:T(8,128)(2,1)S(1)} %get-tuple-element.29.sib_part_ref), custom_call_target="tpu_custom_call" | custom-call | tf_op jit(solution)/shard_map/rest/pallas_call | solution.py:328
  31.8 10.7 %collective-permute-done.12.refs_1_ = bf16[48,1024]{1,0:T(8,128)(2,1)S(1)} collective-permute-done((bf16[48,1024]{1,0:T(8,128)(2,1)S(1)}, bf16[48,1024]{1,0:T(8,128)(2,1)S(1)}, u32[]{:S(2)}, u32[]{:S(2)}) %collective-permute-start.12) | collective-permute-done | bytes 98336 | tf_op jit(solution)/shard_map/ppermute | solution.py:221
  42.5 0.7 %finish.4.refs_2_ = bf16[48,8192]{1,0:T(8,128)(2,1)} custom-call(bf16[48,1024]{1,0:T(8,128)(2,1)S(1)} %get-tuple-element.31.refs_0_, bf16[48,1024]{1,0:T(8,128)(2,1)S(1)} %collective-permute-done.12.refs_1_), custom_call_target="tpu_custom_call" | custom-call | tf_op jit(solution)/shard_map/finish/pallas_call | solution.py:337
  43.2 0.0 collective-permute-done.11.refs_1_
  43.2 0.7 %finish.5.refs_2_ = bf16[48,8192]{1,0:T(8,128)(2,1)} custom-call(bf16[48,2048]{1,0:T(8,128)(2,1)S(1)} %get-tuple-element.30.refs_0_, bf16[48,2048]{1,0:T(8,128)(2,1)S(1)} %collective-permute-done.11.refs_1_, bf16[48,8192]{1,0:T(8,128)(2,1)} %finish.4.refs_2_), custom_call_target="tpu_custom_call", output_to_operand_aliasing={{}: (2, {})} | custom-call | tf_op jit(solution)/shard_map/finish/pallas_call | solution.py:337
  44.0 0.0 collective-permute-done.10.refs_1_
  44.0 0.8 %finish.6.refs_2_ = bf16[48,8192]{1,0:T(8,128)(2,1)} custom-call(bf16[48,2560]{1,0:T(8,128)(2,1)S(1)} %get-tuple-element.27.refs_0_, bf16[48,2560]{1,0:T(8,128)(2,1)S(1)} %collective-permute-done.10.refs_1_, bf16[48,8192]{1,0:T(8,128)(2,1)} %finish.5.refs_2_), custom_call_target="tpu_custom_call", output_to_operand_aliasing={{}: (2, {})} | custom-call | tf_op jit(solution)/shard_map/finish/pallas_call | solution.py:337
  44.7 0.0 collective-permute-done.9.refs_1_
  44.7 0.8 %finish.7 = bf16[48,8192]{1,0:T(8,128)(2,1)} custom-call(bf16[48,2560]{1,0:T(8,128)(2,1)S(1)} %get-tuple-element.25.refs_0_, bf16[48,2560]{1,0:T(8,128)(2,1)S(1)} %collective-permute-done.9.refs_1_, bf16[48,8192]{1,0:T(8,128)(2,1)} %finish.6.refs_2_), custom_call_target="tpu_custom_call", output_to_operand_aliasing={{}: (2, {})} | custom-call | tf_op jit(solution)/shard_map/finish/pallas_call | solution.py:337
  (1 shorter events, 0.0 us)
Async XLA Ops:
  0.0 17.7 %collective-permute-start = (bf16[512,8192]{1,0:T(8,128)(2,1)}, bf16[512,8192]{1,0:T(8,128)(2,1)}, u32[]{:S(2)}, u32[]{:S(2)}) collective-permute-start(bf16[512,8192]{1,0:T(8,128)(2,1)} %own_w_ref.5), channel_id=1, source_target_pairs={{0,1},{1,0},{2,3},{3,2},{4,5},{5,4},{6,7},{7,6},{8,9},{9,8},{10,11... | collective-permute-start | bytes 25165832 | tf_op jit(solution)/shard_map/ppermute | solution.py:221
  1.3 10.3 %collective-permute-start.5 = (bf16[192,256]{1,0:T(8,128)(2,1)S(1)}, bf16[192,256]{1,0:T(8,128)(2,1)S(1)}, u32[]{:S(2)}, u32[]{:S(2)}) collective-permute-start(bf16[192,256]{1,0:T(8,128)(2,1)S(1)} %pad_maximum_fusion.refs_0_), channel_id=1, source_target_pairs={{0,4},{1,5},{2,6},{3,7},{4,0},{5,1},{6,2},{7,3},{8,12},{9,13},{10,... | collective-permute-start | bytes 294920 | tf_op jit(solution)/shard_map/ppermute | solution.py:221
  3.9 8.2 %collective-permute-start.4 = (bf16[192,256]{1,0:T(8,128)(2,1)S(1)}, bf16[192,256]{1,0:T(8,128)(2,1)S(1)}, u32[]{:S(2)}, u32[]{:S(2)}) collective-permute-start(bf16[192,256]{1,0:T(8,128)(2,1)S(1)} %pad_maximum_fusion.refs_0_), channel_id=1, source_target_pairs={{0,8},{1,13},{2,10},{3,15},{4,12},{5,9},{6,14},{7,11},{8,0},{9,5},... | collective-permute-start | bytes 294920 | tf_op jit(solution)/shard_map/ppermute | solution.py:221
  5.5 10.8 %collective-permute-start.3 = (bf16[192,256]{1,0:T(8,128)(2,1)S(1)}, bf16[192,256]{1,0:T(8,128)(2,1)S(1)}, u32[]{:S(2)}, u32[]{:S(2)}) collective-permute-start(bf16[192,256]{1,0:T(8,128)(2,1)S(1)} %pad_maximum_fusion.refs_0_), channel_id=1, source_target_pairs={{0,16},{1,21},{2,18},{3,23},{4,20},{5,17},{6,22},{7,19},{8,24},{9,... | collective-permute-start | bytes 294920 | tf_op jit(solution)/shard_map/ppermute | solution.py:221
  8.0 8.2 %collective-permute-start.2 = (bf16[192,256]{1,0:T(8,128)(2,1)S(1)}, bf16[192,256]{1,0:T(8,128)(2,1)S(1)}, u32[]{:S(2)}, u32[]{:S(2)}) collective-permute-start(bf16[192,256]{1,0:T(8,128)(2,1)S(1)} %pad_maximum_fusion.refs_0_), channel_id=1, source_target_pairs={{0,24},{1,29},{2,26},{3,31},{4,28},{5,25},{6,30},{7,27},{8,16},{9,... | collective-permute-start | bytes 294920 | tf_op jit(solution)/shard_map/ppermute | solution.py:221
  8.3 0.7 %copy-start = (s32[1536]{0:T(1024)S(1)}, s32[1536]{0:T(1024)}, u32[]{:S(2)}) copy-start(s32[1536]{0:T(1024)} %positions_ref.1) | copy-start | bytes 18436
  11.7 5.1 %collective-permute-start.1 = (bf16[96,512]{1,0:T(8,128)(2,1)S(1)}, bf16[96,512]{1,0:T(8,128)(2,1)S(1)}, u32[]{:S(2)}, u32[]{:S(2)}) collective-permute-start(bf16[96,512]{1,0:T(8,128)(2,1)S(1)} %get-tuple-element.21), channel_id=1, source_target_pairs={{0,1},{1,0},{2,3},{3,2},{4,5},{5,4},{6,7},{7,6},{8,9},{9,8},{10,11... | collective-permute-start | bytes 294920 | tf_op jit(solution)/shard_map/ppermute | solution.py:221
  12.1 4.6 %collective-permute-start.8 = (bf16[192,256]{1,0:T(8,128)(2,1)S(1)}, bf16[192,256]{1,0:T(8,128)(2,1)S(1)}, u32[]{:S(2)}, u32[]{:S(2)}) collective-permute-start(bf16[192,256]{1,0:T(8,128)(2,1)S(1)} %collective-permute-done.4.refs_3_), channel_id=1, source_target_pairs={{0,1},{1,0},{2,3},{3,2},{4,5},{5,4},{6,7},{7,6},{8,9},{9,8},{10,11... | collective-permute-start | bytes 294920 | tf_op jit(solution)/shard_map/ppermute | solution.py:221
  16.2 1.3 %collective-permute-start.7 = (bf16[192,256]{1,0:T(8,128)(2,1)S(1)}, bf16[192,256]{1,0:T(8,128)(2,1)S(1)}, u32[]{:S(2)}, u32[]{:S(2)}) collective-permute-start(bf16[192,256]{1,0:T(8,128)(2,1)S(1)} %collective-permute-done.3.refs_2_), channel_id=1, source_target_pairs={{0,1},{1,0},{2,3},{3,2},{4,5},{5,4},{6,7},{7,6},{8,9},{9,8},{10,11... | collective-permute-start | bytes 294920 | tf_op jit(solution)/shard_map/ppermute | solution.py:221
  16.2 1.5 %collective-permute-start.6 = (bf16[192,256]{1,0:T(8,128)(2,1)S(1)}, bf16[192,256]{1,0:T(8,128)(2,1)S(1)}, u32[]{:S(2)}, u32[]{:S(2)}) collective-permute-start(bf16[192,256]{1,0:T(8,128)(2,1)S(1)} %collective-permute-done.2.refs_1_), channel_id=1, source_target_pairs={{0,1},{1,0},{2,3},{3,2},{4,5},{5,4},{6,7},{7,6},{8,9},{9,8},{10,11... | collective-permute-start | bytes 294920 | tf_op jit(solution)/shard_map/ppermute | solution.py:221
  22.6 21.3 %collective-permute-start.10 = (bf16[48,2560]{1,0:T(8,128)(2,1)S(1)}, bf16[48,2560]{1,0:T(8,128)(2,1)S(1)}, u32[]{:S(2)}, u32[]{:S(2)}) collective-permute-start(bf16[48,2560]{1,0:T(8,128)(2,1)S(1)} %get-tuple-element.28), channel_id=1, source_target_pairs={{0,2},{1,3},{2,0},{3,1},{4,6},{5,7},{6,4},{7,5},{8,10},{9,11},{10,... | collective-permute-start | bytes 737288 | tf_op jit(solution)/shard_map/ppermute | solution.py:221
  27.1 17.6 %collective-permute-start.9 = (bf16[48,2560]{1,0:T(8,128)(2,1)S(1)}, bf16[48,2560]{1,0:T(8,128)(2,1)S(1)}, u32[]{:S(2)}, u32[]{:S(2)}) collective-permute-start(bf16[48,2560]{1,0:T(8,128)(2,1)S(1)} %get-tuple-element.26), channel_id=1, source_target_pairs={{0,2},{1,3},{2,0},{3,1},{4,6},{5,7},{6,4},{7,5},{8,10},{9,11},{10,... | collective-permute-start | bytes 737288 | tf_op jit(solution)/shard_map/ppermute | solution.py:221
  28.5 14.7 %collective-permute-start.11 = (bf16[48,2048]{1,0:T(8,128)(2,1)S(1)}, bf16[48,2048]{1,0:T(8,128)(2,1)S(1)}, u32[]{:S(2)}, u32[]{:S(2)}) collective-permute-start(bf16[48,2048]{1,0:T(8,128)(2,1)S(1)} %again.1), channel_id=1, source_target_pairs={{0,2},{1,3},{2,0},{3,1},{4,6},{5,7},{6,4},{7,5},{8,10},{9,11},{10,... | collective-permute-start | bytes 589832 | tf_op jit(solution)/shard_map/ppermute | solution.py:221
  30.1 12.4 %collective-permute-start.12 = (bf16[48,1024]{1,0:T(8,128)(2,1)S(1)}, bf16[48,1024]{1,0:T(8,128)(2,1)S(1)}, u32[]{:S(2)}, u32[]{:S(2)}) collective-permute-start(bf16[48,1024]{1,0:T(8,128)(2,1)S(1)} %get-tuple-element.32), channel_id=1, source_target_pairs={{0,2},{1,3},{2,0},{3,1},{4,6},{5,7},{6,4},{7,5},{8,10},{9,11},{10,... | collective-permute-start | bytes 294920 | tf_op jit(solution)/shard_map/ppermute | solution.py:221

commit v2 on v1

--- a/solution.py
+++ b/solution.py
@@ -203,7 +203,11 @@
 
 
 def pairing(cp_size):
-    return [(o, o + 1) for o in range(cp_size - 2, 0, -2)]
+    half = cp_size // 2
+    others = [o for o in range(2, cp_size, 2) if o != half]
+    even = [half] + others
+    odd = [half + 1] + [o + 1 for o in others[::-1]]
+    return list(zip(even, odd))
 
 
 def shards(cp_size, tp_size, queries, keys, values, positions, out_weight):

time: 45.8 us -> 46 us (level)
  no operation moved by 1% of the time
where the time goes in v2:
time: 46 us; the launch traced here: 45.7 us
  waiting for transfers between devices  16 us (35%)
  Pallas kernels  15.5 us (34%)
  starting transfers between devices  12.6 us (27%)
  local copies, waits for them, and re-layouts  1.53 us (3%)
    ppermute x13, waiting for transfers between devices, permute(): return lax.ppermute(x, AXES, pairs)  16 us
    ppermute x13, starting transfers between devices, permute(): return lax.ppermute(x, AXES, pairs)  12.6 us
    pallas_call x2, Pallas kernels, call(): pl.pallas_call(kernel, in_specs=in_specs, out_shape=out_shape, scratch_sh...  5.87 us
    pallas_call x4, Pallas kernels, shards(): pl.pallas_call(functools.partial(finish_kernel, lo), in_specs=[whole, who...  2.94 us
    pallas_call x1, Pallas kernels, shards(): pl.pallas_call(functools.partial(prepare_kernel, offsets), in_specs=[pl.B...  2.71 us
    pallas_call x1, Pallas kernels, shards(): pl.pallas_call(functools.partial(send_kernel, stack), in_specs=[whole] *...  1.94 us
    pallas_call x1, Pallas kernels, shards(): pl.pallas_call(functools.partial(resident_kernel, 0), in_specs=[whole] *...  1.18 us
  transfers between devices with their start and end apart: 13, of which 4 were waited for; matrix products, arithmetic and copies ran while one was open for 2% of the time, Pallas kernels for 21%

profile of v2, /device:TPU:0, one launch (start us, length us, event | category | flops | bytes accessed | tf_op | source)
XLA Modules:
  0.0 45.7 jit_solution(3954087238860123807)
XLA Ops:
  0.0 0.5 %collective-permute-start = (bf16[512,8192]{1,0:T(8,128)(2,1)}, bf16[512,8192]{1,0:T(8,128)(2,1)}, u32[]{:S(2)}, u32[]{:S(2)}) collective-permute-start(bf16[512,8192]{1,0:T(8,128)(2,1)} %own_w_ref.5), channel_id=1, source_target_pairs={{0,1},{1,0},{2,3},{3,2},{4,5},{5,4},{6,7},{7,6},{8,9},{9,8},{10,11... | collective-permute-start | bytes 25165832 | tf_op jit(solution)/shard_map/ppermute | solution.py:225
  0.5 0.8 %constant_dynamic-slice_fusion = (bf16[192,128]{1,0:T(8,128)(2,1)S(1)}, bf16[192,128]{1,0:T(8,128)(2,1)S(1)}) fusion(bf16[192,256]{1,0:T(8,128)(2,1)} %param.7, s32[]{:T(128)S(6)} %select_n.10, bf16[192,256]{1,0:T(8,128)(2,1)} %param.6), kind=kLoop, calls=%fused_computation.1 | loop fusion | bytes 196612 | tf_op jit(solution)/shard_map/dynamic_slice | solution.py:232
  1.3 2.5 %collective-permute-start.5 = (bf16[192,256]{1,0:T(8,128)(2,1)S(1)}, bf16[192,256]{1,0:T(8,128)(2,1)S(1)}, u32[]{:S(2)}, u32[]{:S(2)}) collective-permute-start(bf16[192,256]{1,0:T(8,128)(2,1)S(1)} %pad_maximum_fusion.refs_0_), channel_id=1, source_target_pairs={{0,4},{1,5},{2,6},{3,7},{4,0},{5,1},{6,2},{7,3},{8,12},{9,13},{10,... | collective-permute-start | bytes 294920 | tf_op jit(solution)/shard_map/ppermute | solution.py:225
  3.9 3.6 %collective-permute-start.4 = (bf16[192,256]{1,0:T(8,128)(2,1)S(1)}, bf16[192,256]{1,0:T(8,128)(2,1)S(1)}, u32[]{:S(2)}, u32[]{:S(2)}) collective-permute-start(bf16[192,256]{1,0:T(8,128)(2,1)S(1)} %pad_maximum_fusion.refs_0_), channel_id=1, source_target_pairs={{0,24},{1,13},{2,26},{3,15},{4,28},{5,9},{6,30},{7,11},{8,16},{9,5... | collective-permute-start | bytes 294920 | tf_op jit(solution)/shard_map/ppermute | solution.py:225
  7.5 0.0 collective-permute-start.3
  7.5 0.8 %collective-permute-start.2 = (bf16[192,256]{1,0:T(8,128)(2,1)S(1)}, bf16[192,256]{1,0:T(8,128)(2,1)S(1)}, u32[]{:S(2)}, u32[]{:S(2)}) collective-permute-start(bf16[192,256]{1,0:T(8,128)(2,1)S(1)} %pad_maximum_fusion.refs_0_), channel_id=1, source_target_pairs={{0,16},{1,21},{2,18},{3,23},{4,20},{5,17},{6,22},{7,19},{8,24},{9,... | collective-permute-start | bytes 294920 | tf_op jit(solution)/shard_map/ppermute | solution.py:225
  8.3 0.0 copy-start
  8.3 0.7 %copy-done = s32[1536]{0:T(1024)S(1)} copy-done((s32[1536]{0:T(1024)S(1)}, s32[1536]{0:T(1024)}, u32[]{:S(2)}) %copy-start) | copy-done | bytes 6168
  9.0 2.7 %prepare.1 = (f32[96,1536]{1,0:T(8,128)S(1)}, bf16[96,512]{1,0:T(8,128)(2,1)S(1)}, bf16[96,512]{1,0:T(8,128)(2,1)S(1)}, bf16[512,3072]{1,0:T(8,128)(2,1)S(1)}) custom-call(s32[1536]{0:T(1024)S(1)} %copy-done, bf16[192,512]{1,0:T(8,128)(2,1)} %queries_ref.1, bf16[512,8192]{1,0:T(8,128)(2,1)} %own_w_ref.5), custom_call_target="tpu_custom_call" | custom-call | tf_op jit(solution)/shard_map/prepare/pallas_call | solution.py:260
  11.7 0.0 collective-permute-done.5.refs_4_
  11.7 0.4 collective-permute-start.1
  12.1 0.0 collective-permute-done.4.refs_3_
  12.1 0.2 collective-permute-start.8
  12.3 1.0 %collective-permute-done.3.refs_2_ = bf16[192,256]{1,0:T(8,128)(2,1)S(1)} collective-permute-done((bf16[192,256]{1,0:T(8,128)(2,1)S(1)}, bf16[192,256]{1,0:T(8,128)(2,1)S(1)}, u32[]{:S(2)}, u32[]{:S(2)}) %collective-permute-start.3) | collective-permute-done | bytes 98336 | tf_op jit(solution)/shard_map/ppermute | solution.py:225
  13.3 0.0 collective-permute-start.7
  13.3 3.3 %collective-permute-done.2.refs_1_ = bf16[192,256]{1,0:T(8,128)(2,1)S(1)} collective-permute-done((bf16[192,256]{1,0:T(8,128)(2,1)S(1)}, bf16[192,256]{1,0:T(8,128)(2,1)S(1)}, u32[]{:S(2)}, u32[]{:S(2)}) %collective-permute-start.2) | collective-permute-done | bytes 98336 | tf_op jit(solution)/shard_map/ppermute | solution.py:225
  16.6 0.4 collective-permute-start.6
  17.0 0.0 collective-permute-done.1.sib_ref
  17.0 0.0 collective-permute-done.8.refs_7_
  17.0 0.0 collective-permute-done.7.refs_6_
  17.0 0.9 %collective-permute-done.6.refs_5_ = bf16[192,256]{1,0:T(8,128)(2,1)S(1)} collective-permute-done((bf16[192,256]{1,0:T(8,128)(2,1)S(1)}, bf16[192,256]{1,0:T(8,128)(2,1)S(1)}, u32[]{:S(2)}, u32[]{:S(2)}) %collective-permute-start.6) | collective-permute-done | bytes 98336 | tf_op jit(solution)/shard_map/ppermute | solution.py:225
  17.9 0.0 collective-permute-done.sib_w_ref
  17.9 1.9 %send.1 = (bf16[48,1024]{1,0:T(8,128)(2,1)S(1)}, bf16[48,1024]{1,0:T(8,128)(2,1)S(1)}, bf16[512,3072]{1,0:T(8,128)(2,1)S(1)}) custom-call(f32[96,1536]{1,0:T(8,128)S(1)} %get-tuple-element.19.bias_ref, bf16[96,512]{1,0:T(8,128)(2,1)S(1)} %get-tuple-element.20.own_ref, bf16[96,512]{1,0:T(8,128)(2,1)S(1)} %collective-permute-done.1.sib_ref, ...), custom_call_target="tpu_custom_call" | custom-call | tf_op jit(solution)/shard_map/send/pallas_call | solution.py:296
  19.9 3.0 %shard_map.55 = (bf16[48,1024]{1,0:T(8,128)(2,1)S(1)}, bf16[48,2560]{1,0:T(8,128)(2,1)S(1)}, bf16[48,2560]{1,0:T(8,128)(2,1)S(1)}) custom-call(f32[96,1536]{1,0:T(8,128)S(1)} %get-tuple-element.19.bias_ref, bf16[96,512]{1,0:T(8,128)(2,1)S(1)} %get-tuple-element.20.own_ref, bf16[96,512]{1,0:T(8,128)(2,1)S(1)} %collective-permute-done.1.sib_ref, ...), custom_call_target="tpu_custom_call" | custom-call | tf_op jit(solution)/shard_map/pallas_call | solution.py:278
  22.8 1.6 %collective-permute-start.10 = (bf16[48,2560]{1,0:T(8,128)(2,1)S(1)}, bf16[48,2560]{1,0:T(8,128)(2,1)S(1)}, u32[]{:S(2)}, u32[]{:S(2)}) collective-permute-start(bf16[48,2560]{1,0:T(8,128)(2,1)S(1)} %get-tuple-element.28), channel_id=1, source_target_pairs={{0,2},{1,3},{2,0},{3,1},{4,6},{5,7},{6,4},{7,5},{8,10},{9,11},{10,... | collective-permute-start | bytes 737288 | tf_op jit(solution)/shard_map/ppermute | solution.py:225
  24.4 2.9 %shard_map.56 = (bf16[48,2560]{1,0:T(8,128)(2,1)S(1)}, bf16[48,2560]{1,0:T(8,128)(2,1)S(1)}) custom-call(bf16[512,8192]{1,0:T(8,128)(2,1)} %own_w_ref.5, bf16[512,8192]{1,0:T(8,128)(2,1)} %collective-permute-done.sib_w_ref, bf16[48,1024]{1,0:T(8,128)(2,1)S(1)} %get-tuple-element.24.refs_0_.attended_ref, ...), custom_call_target="tpu_custom_call" | custom-call | tf_op jit(solution)/shard_map/pallas_call | solution.py:278
  27.3 0.6 %collective-permute-start.9 = (bf16[48,2560]{1,0:T(8,128)(2,1)S(1)}, bf16[48,2560]{1,0:T(8,128)(2,1)S(1)}, u32[]{:S(2)}, u32[]{:S(2)}) collective-permute-start(bf16[48,2560]{1,0:T(8,128)(2,1)S(1)} %get-tuple-element.26), channel_id=1, source_target_pairs={{0,2},{1,3},{2,0},{3,1},{4,6},{5,7},{6,4},{7,5},{8,10},{9,11},{10,... | collective-permute-start | bytes 737288 | tf_op jit(solution)/shard_map/ppermute | solution.py:225
  27.9 0.8 %again.1 = bf16[48,2048]{1,0:T(8,128)(2,1)S(1)} custom-call(bf16[48,1024]{1,0:T(8,128)(2,1)S(1)} %get-tuple-element.23.sent_ref.refs_1_.attended_ref, bf16[512,3072]{1,0:T(8,128)(2,1)S(1)} %get-tuple-element.22.own_part_ref, bf16[512,3072]{1,0:T(8,128)(2,1)S(1)} %get-tuple-element.29.sib_part_ref), custom_call_target="tpu_custom_call" | custom-call | tf_op jit(solution)/shard_map/again/pallas_call | solution.py:306
  28.7 1.6 %collective-permute-start.11 = (bf16[48,2048]{1,0:T(8,128)(2,1)S(1)}, bf16[48,2048]{1,0:T(8,128)(2,1)S(1)}, u32[]{:S(2)}, u32[]{:S(2)}) collective-permute-start(bf16[48,2048]{1,0:T(8,128)(2,1)S(1)} %again.1), channel_id=1, source_target_pairs={{0,2},{1,3},{2,0},{3,1},{4,6},{5,7},{6,4},{7,5},{8,10},{9,11},{10,... | collective-permute-start | bytes 589832 | tf_op jit(solution)/shard_map/ppermute | solution.py:225
  30.3 0.5 %collective-permute-start.12 = (bf16[48,1024]{1,0:T(8,128)(2,1)S(1)}, bf16[48,1024]{1,0:T(8,128)(2,1)S(1)}, u32[]{:S(2)}, u32[]{:S(2)}) collective-permute-start(bf16[48,1024]{1,0:T(8,128)(2,1)S(1)} %get-tuple-element.32), channel_id=1, source_target_pairs={{0,2},{1,3},{2,0},{3,1},{4,6},{5,7},{6,4},{7,5},{8,10},{9,11},{10,... | collective-permute-start | bytes 294920 | tf_op jit(solution)/shard_map/ppermute | solution.py:225
  30.8 1.2 %rest.1 = (bf16[48,1024]{1,0:T(8,128)(2,1)S(1)}, bf16[48,2048]{1,0:T(8,128)(2,1)S(1)}) custom-call(bf16[48,1024]{1,0:T(8,128)(2,1)S(1)} %get-tuple-element.24.refs_0_.attended_ref, bf16[512,3072]{1,0:T(8,128)(2,1)S(1)} %get-tuple-element.22.own_part_ref, bf16[512,3072]{1,0:T(8,128)(2,1)S(1)} %get-tuple-element.29.sib_part_ref), custom_call_target="tpu_custom_call" | custom-call | tf_op jit(solution)/shard_map/rest/pallas_call | solution.py:332
  32.0 10.7 %collective-permute-done.12.refs_1_ = bf16[48,1024]{1,0:T(8,128)(2,1)S(1)} collective-permute-done((bf16[48,1024]{1,0:T(8,128)(2,1)S(1)}, bf16[48,1024]{1,0:T(8,128)(2,1)S(1)}, u32[]{:S(2)}, u32[]{:S(2)}) %collective-permute-start.12) | collective-permute-done | bytes 98336 | tf_op jit(solution)/shard_map/ppermute | solution.py:225
  42.7 0.7 %finish.4.refs_2_ = bf16[48,8192]{1,0:T(8,128)(2,1)} custom-call(bf16[48,1024]{1,0:T(8,128)(2,1)S(1)} %get-tuple-element.31.refs_0_, bf16[48,1024]{1,0:T(8,128)(2,1)S(1)} %collective-permute-done.12.refs_1_), custom_call_target="tpu_custom_call" | custom-call | tf_op jit(solution)/shard_map/finish/pallas_call | solution.py:341
  43.4 0.0 collective-permute-done.11.refs_1_
  43.4 0.7 %finish.5.refs_2_ = bf16[48,8192]{1,0:T(8,128)(2,1)} custom-call(bf16[48,2048]{1,0:T(8,128)(2,1)S(1)} %get-tuple-element.30.refs_0_, bf16[48,2048]{1,0:T(8,128)(2,1)S(1)} %collective-permute-done.11.refs_1_, bf16[48,8192]{1,0:T(8,128)(2,1)} %finish.4.refs_2_), custom_call_target="tpu_custom_call", output_to_operand_aliasing={{}: (2, {})} | custom-call | tf_op jit(solution)/shard_map/finish/pallas_call | solution.py:341
  44.2 0.0 collective-permute-done.10.refs_1_
  44.2 0.8 %finish.6.refs_2_ = bf16[48,8192]{1,0:T(8,128)(2,1)} custom-call(bf16[48,2560]{1,0:T(8,128)(2,1)S(1)} %get-tuple-element.27.refs_0_, bf16[48,2560]{1,0:T(8,128)(2,1)S(1)} %collective-permute-done.10.refs_1_, bf16[48,8192]{1,0:T(8,128)(2,1)} %finish.5.refs_2_), custom_call_target="tpu_custom_call", output_to_operand_aliasing={{}: (2, {})} | custom-call | tf_op jit(solution)/shard_map/finish/pallas_call | solution.py:341
  44.9 0.0 collective-permute-done.9.refs_1_
  44.9 0.8 %finish.7 = bf16[48,8192]{1,0:T(8,128)(2,1)} custom-call(bf16[48,2560]{1,0:T(8,128)(2,1)S(1)} %get-tuple-element.25.refs_0_, bf16[48,2560]{1,0:T(8,128)(2,1)S(1)} %collective-permute-done.9.refs_1_, bf16[48,8192]{1,0:T(8,128)(2,1)} %finish.6.refs_2_), custom_call_target="tpu_custom_call", output_to_operand_aliasing={{}: (2, {})} | custom-call | tf_op jit(solution)/shard_map/finish/pallas_call | solution.py:341
  (1 shorter events, 0.0 us)
Async XLA Ops:
  0.0 17.9 %collective-permute-start = (bf16[512,8192]{1,0:T(8,128)(2,1)}, bf16[512,8192]{1,0:T(8,128)(2,1)}, u32[]{:S(2)}, u32[]{:S(2)}) collective-permute-start(bf16[512,8192]{1,0:T(8,128)(2,1)} %own_w_ref.5), channel_id=1, source_target_pairs={{0,1},{1,0},{2,3},{3,2},{4,5},{5,4},{6,7},{7,6},{8,9},{9,8},{10,11... | collective-permute-start | bytes 25165832 | tf_op jit(solution)/shard_map/ppermute | solution.py:225
  1.3 10.3 %collective-permute-start.5 = (bf16[192,256]{1,0:T(8,128)(2,1)S(1)}, bf16[192,256]{1,0:T(8,128)(2,1)S(1)}, u32[]{:S(2)}, u32[]{:S(2)}) collective-permute-start(bf16[192,256]{1,0:T(8,128)(2,1)S(1)} %pad_maximum_fusion.refs_0_), channel_id=1, source_target_pairs={{0,4},{1,5},{2,6},{3,7},{4,0},{5,1},{6,2},{7,3},{8,12},{9,13},{10,... | collective-permute-start | bytes 294920 | tf_op jit(solution)/shard_map/ppermute | solution.py:225
  3.9 8.2 %collective-permute-start.4 = (bf16[192,256]{1,0:T(8,128)(2,1)S(1)}, bf16[192,256]{1,0:T(8,128)(2,1)S(1)}, u32[]{:S(2)}, u32[]{:S(2)}) collective-permute-start(bf16[192,256]{1,0:T(8,128)(2,1)S(1)} %pad_maximum_fusion.refs_0_), channel_id=1, source_target_pairs={{0,24},{1,13},{2,26},{3,15},{4,28},{5,9},{6,30},{7,11},{8,16},{9,5... | collective-permute-start | bytes 294920 | tf_op jit(solution)/shard_map/ppermute | solution.py:225
  7.5 5.8 %collective-permute-start.3 = (bf16[192,256]{1,0:T(8,128)(2,1)S(1)}, bf16[192,256]{1,0:T(8,128)(2,1)S(1)}, u32[]{:S(2)}, u32[]{:S(2)}) collective-permute-start(bf16[192,256]{1,0:T(8,128)(2,1)S(1)} %pad_maximum_fusion.refs_0_), channel_id=1, source_target_pairs={{0,8},{1,29},{2,10},{3,31},{4,12},{5,25},{6,14},{7,27},{8,0},{9,21... | collective-permute-start | bytes 294920 | tf_op jit(solution)/shard_map/ppermute | solution.py:225
  7.5 9.1 %collective-permute-start.2 = (bf16[192,256]{1,0:T(8,128)(2,1)S(1)}, bf16[192,256]{1,0:T(8,128)(2,1)S(1)}, u32[]{:S(2)}, u32[]{:S(2)}) collective-permute-start(bf16[192,256]{1,0:T(8,128)(2,1)S(1)} %pad_maximum_fusion.refs_0_), channel_id=1, source_target_pairs={{0,16},{1,21},{2,18},{3,23},{4,20},{5,17},{6,22},{7,19},{8,24},{9,... | collective-permute-start | bytes 294920 | tf_op jit(solution)/shard_map/ppermute | solution.py:225
  8.3 0.7 %copy-start = (s32[1536]{0:T(1024)S(1)}, s32[1536]{0:T(1024)}, u32[]{:S(2)}) copy-start(s32[1536]{0:T(1024)} %positions_ref.1) | copy-start | bytes 18436
  11.7 5.3 %collective-permute-start.1 = (bf16[96,512]{1,0:T(8,128)(2,1)S(1)}, bf16[96,512]{1,0:T(8,128)(2,1)S(1)}, u32[]{:S(2)}, u32[]{:S(2)}) collective-permute-start(bf16[96,512]{1,0:T(8,128)(2,1)S(1)} %get-tuple-element.21), channel_id=1, source_target_pairs={{0,1},{1,0},{2,3},{3,2},{4,5},{5,4},{6,7},{7,6},{8,9},{9,8},{10,11... | collective-permute-start | bytes 294920 | tf_op jit(solution)/shard_map/ppermute | solution.py:225
  12.1 4.9 %collective-permute-start.8 = (bf16[192,256]{1,0:T(8,128)(2,1)S(1)}, bf16[192,256]{1,0:T(8,128)(2,1)S(1)}, u32[]{:S(2)}, u32[]{:S(2)}) collective-permute-start(bf16[192,256]{1,0:T(8,128)(2,1)S(1)} %collective-permute-done.4.refs_3_), channel_id=1, source_target_pairs={{0,1},{1,0},{2,3},{3,2},{4,5},{5,4},{6,7},{7,6},{8,9},{9,8},{10,11... | collective-permute-start | bytes 294920 | tf_op jit(solution)/shard_map/ppermute | solution.py:225
  13.3 3.7 %collective-permute-start.7 = (bf16[192,256]{1,0:T(8,128)(2,1)S(1)}, bf16[192,256]{1,0:T(8,128)(2,1)S(1)}, u32[]{:S(2)}, u32[]{:S(2)}) collective-permute-start(bf16[192,256]{1,0:T(8,128)(2,1)S(1)} %collective-permute-done.3.refs_2_), channel_id=1, source_target_pairs={{0,1},{1,0},{2,3},{3,2},{4,5},{5,4},{6,7},{7,6},{8,9},{9,8},{10,11... | collective-permute-start | bytes 294920 | tf_op jit(solution)/shard_map/ppermute | solution.py:225
  16.6 1.3 %collective-permute-start.6 = (bf16[192,256]{1,0:T(8,128)(2,1)S(1)}, bf16[192,256]{1,0:T(8,128)(2,1)S(1)}, u32[]{:S(2)}, u32[]{:S(2)}) collective-permute-start(bf16[192,256]{1,0:T(8,128)(2,1)S(1)} %collective-permute-done.2.refs_1_), channel_id=1, source_target_pairs={{0,1},{1,0},{2,3},{3,2},{4,5},{5,4},{6,7},{7,6},{8,9},{9,8},{10,11... | collective-permute-start | bytes 294920 | tf_op jit(solution)/shard_map/ppermute | solution.py:225
  22.8 21.3 %collective-permute-start.10 = (bf16[48,2560]{1,0:T(8,128)(2,1)S(1)}, bf16[48,2560]{1,0:T(8,128)(2,1)S(1)}, u32[]{:S(2)}, u32[]{:S(2)}) collective-permute-start(bf16[48,2560]{1,0:T(8,128)(2,1)S(1)} %get-tuple-element.28), channel_id=1, source_target_pairs={{0,2},{1,3},{2,0},{3,1},{4,6},{5,7},{6,4},{7,5},{8,10},{9,11},{10,... | collective-permute-start | bytes 737288 | tf_op jit(solution)/shard_map/ppermute | solution.py:225
  27.3 17.6 %collective-permute-start.9 = (bf16[48,2560]{1,0:T(8,128)(2,1)S(1)}, bf16[48,2560]{1,0:T(8,128)(2,1)S(1)}, u32[]{:S(2)}, u32[]{:S(2)}) collective-permute-start(bf16[48,2560]{1,0:T(8,128)(2,1)S(1)} %get-tuple-element.26), channel_id=1, source_target_pairs={{0,2},{1,3},{2,0},{3,1},{4,6},{5,7},{6,4},{7,5},{8,10},{9,11},{10,... | collective-permute-start | bytes 737288 | tf_op jit(solution)/shard_map/ppermute | solution.py:225
  28.7 14.7 %collective-permute-start.11 = (bf16[48,2048]{1,0:T(8,128)(2,1)S(1)}, bf16[48,2048]{1,0:T(8,128)(2,1)S(1)}, u32[]{:S(2)}, u32[]{:S(2)}) collective-permute-start(bf16[48,2048]{1,0:T(8,128)(2,1)S(1)} %again.1), channel_id=1, source_target_pairs={{0,2},{1,3},{2,0},{3,1},{4,6},{5,7},{6,4},{7,5},{8,10},{9,11},{10,... | collective-permute-start | bytes 589832 | tf_op jit(solution)/shard_map/ppermute | solution.py:225
  30.3 12.4 %collective-permute-start.12 = (bf16[48,1024]{1,0:T(8,128)(2,1)S(1)}, bf16[48,1024]{1,0:T(8,128)(2,1)S(1)}, u32[]{:S(2)}, u32[]{:S(2)}) collective-permute-start(bf16[48,1024]{1,0:T(8,128)(2,1)S(1)} %get-tuple-element.32), channel_id=1, source_target_pairs={{0,2},{1,3},{2,0},{3,1},{4,6},{5,7},{6,4},{7,5},{8,10},{9,11},{10,... | collective-permute-start | bytes 294920 | tf_op jit(solution)/shard_map/ppermute | solution.py:225

commit v3 on v2

--- a/solution.py
+++ b/solution.py
@@ -14,7 +14,7 @@
 LOG2E = 1.4426950408889634
 AXES = ("cp", "tp")
 VMEM_LIMIT = 36 * 2**20
-COLUMN_CUTS = (0, 2, 6, 11, 16)
+COLUMN_CUTS = (0, 2, 5, 9, 13, 16)
 TILE = 512
 
 
@@ -26,24 +26,32 @@
     rows = out_ref.shape[0]
     heads = own_ref.shape[1] // HEAD
     at_rows = slice(first_row, first_row + rows)
-    for side, q_ref in enumerate((own_ref, sib_ref)):
-        for first in range(0, heads, stack):
-            q = jnp.concatenate(
-                [q_ref[at_rows, h * HEAD : (h + 1) * HEAD] for h in range(first, first + stack)],
-                axis=0,
-            )
-            scores = lax.dot_general(
-                q, keys, (((1,), (1,)), ((), ())), preferred_element_type=jnp.float32
-            )
-            mask = bias_ref[at_rows, :][None]
-            scores = (scores.reshape(stack, rows, -1) + mask).reshape(scores.shape)
-            top = jnp.max(scores, axis=1, keepdims=True)
-            weights = jnp.exp2((scores - top) * scale).astype(jnp.bfloat16)
-            mixed = jnp.dot(weights, values, preferred_element_type=jnp.float32)
-            result = (mixed[:, :HEAD] / mixed[:, HEAD:]).astype(jnp.bfloat16)
-            for i in range(stack):
-                at = (side * heads + first + i) * HEAD
-                out_ref[:, at : at + HEAD] = result[i * rows : (i + 1) * rows]
+    groups = [(side, first) for side in range(2) for first in range(0, heads, stack)]
+
+    def scores_of(side, first):
+        q_ref = (own_ref, sib_ref)[side]
+        q = jnp.concatenate(
+            [q_ref[at_rows, h * HEAD : (h + 1) * HEAD] for h in range(first, first + stack)],
+            axis=0,
+        )
+        return lax.dot_general(
+            q, keys, (((1,), (1,)), ((), ())), preferred_element_type=jnp.float32
+        )
+
+    ahead = [scores_of(*group) for group in groups[:2]]
+    for n, (side, first) in enumerate(groups):
+        mask = bias_ref[at_rows, :][None]
+        scores = ahead.pop(0)
+        scores = (scores.reshape(stack, rows, -1) + mask).reshape(scores.shape)
+        top = jnp.max(scores, axis=1, keepdims=True)
+        weights = jnp.exp2((scores - top) * scale).astype(jnp.bfloat16)
+        if n + 2 < len(groups):
+            ahead.append(scores_of(*groups[n + 2]))
+        mixed = jnp.dot(weights, values, preferred_element_type=jnp.float32)
+        result = (mixed[:, :HEAD] / mixed[:, HEAD:]).astype(jnp.bfloat16)
+        for i in range(stack):
+            at = (side * heads + first + i) * HEAD
+            out_ref[:, at : at + HEAD] = result[i * rows : (i + 1) * rows]
 
 
 def weight_loads(first, own_w_ref, sib_w_ref, weight_ref, sems):

time: 46 us -> 46.1 us (level)
  waiting for transfers between devices: 16 us -> 13 us
  starting transfers between devices: 12.6 us -> 14.2 us
  Pallas kernels: 15.5 us -> 16.8 us
    ppermute x13 -> x14, waiting for transfers between devices: 16 us -> 13 us  [permute(): return lax.ppermute(x, AXES, pairs)]
    ppermute x13 -> x14, starting transfers between devices: 12.6 us -> 14.2 us  [permute(): return lax.ppermute(x, AXES, pairs)]
    pallas_call x2 -> x3, Pallas kernels: 5.87 us -> 7.32 us  [call(): pl.pallas_call(kernel, in_specs=in_specs, out_shape=out_shape, scratch_sh...]
    pallas_call x4 -> x5, Pallas kernels: 2.94 us -> 3.56 us  [shards(): pl.pallas_call(functools.partial(finish_kernel, lo), in_specs=[whole, who...]
  transfers between devices with their start and end apart: 13 -> 14, of which waited for: 4 -> 4; matrix products, arithmetic and copies ran while one was open for 2% -> 2% of each run, Pallas kernels for 21% -> 26%
where the time goes in v3:
time: 46.1 us; the launch traced here: 45.7 us
  Pallas kernels  16.8 us (36%)
  starting transfers between devices  14.2 us (31%)
  waiting for transfers between devices  13 us (28%)
  local copies, waits for them, and re-layouts  1.53 us (3%)
    ppermute x14, starting transfers between devices, permute(): return lax.ppermute(x, AXES, pairs)  14.2 us
    ppermute x14, waiting for transfers between devices, permute(): return lax.ppermute(x, AXES, pairs)  13 us
    pallas_call x3, Pallas kernels, call(): pl.pallas_call(kernel, in_specs=in_specs, out_shape=out_shape, scratch_sh...  7.32 us
    pallas_call x5, Pallas kernels, shards(): pl.pallas_call(functools.partial(finish_kernel, lo), in_specs=[whole, who...  3.56 us
    pallas_call x1, Pallas kernels, shards(): pl.pallas_call(functools.partial(prepare_kernel, offsets), in_specs=[pl.B...  2.56 us
    pallas_call x1, Pallas kernels, shards(): pl.pallas_call(functools.partial(send_kernel, stack), in_specs=[whole] *...  1.75 us
    pallas_call x1, Pallas kernels, shards(): pl.pallas_call(functools.partial(resident_kernel, 0), in_specs=[whole] *...  0.99 us
  transfers between devices with their start and end apart: 14, of which 4 were waited for; matrix products, arithmetic and copies ran while one was open for 2% of the time, Pallas kernels for 26%

profile of v3, /device:TPU:0, one launch (start us, length us, event | category | flops | bytes accessed | tf_op | source)
XLA Modules:
  0.0 45.7 jit_solution(3129208153325301599)
XLA Ops:
  0.0 0.5 %collective-permute-start = (bf16[512,8192]{1,0:T(8,128)(2,1)}, bf16[512,8192]{1,0:T(8,128)(2,1)}, u32[]{:S(2)}, u32[]{:S(2)}) collective-permute-start(bf16[512,8192]{1,0:T(8,128)(2,1)} %own_w_ref.7), channel_id=1, source_target_pairs={{0,1},{1,0},{2,3},{3,2},{4,5},{5,4},{6,7},{7,6},{8,9},{9,8},{10,11... | collective-permute-start | bytes 25165832 | tf_op jit(solution)/shard_map/ppermute | solution.py:233
  0.5 0.8 %constant_dynamic-slice_fusion = (bf16[192,128]{1,0:T(8,128)(2,1)S(1)}, bf16[192,128]{1,0:T(8,128)(2,1)S(1)}) fusion(bf16[192,256]{1,0:T(8,128)(2,1)} %param.7, s32[]{:T(128)S(6)} %select_n.10, bf16[192,256]{1,0:T(8,128)(2,1)} %param.6), kind=kLoop, calls=%fused_computation.1 | loop fusion | bytes 196612 | tf_op jit(solution)/shard_map/dynamic_slice | solution.py:240
  1.3 2.5 %collective-permute-start.5 = (bf16[192,256]{1,0:T(8,128)(2,1)S(1)}, bf16[192,256]{1,0:T(8,128)(2,1)S(1)}, u32[]{:S(2)}, u32[]{:S(2)}) collective-permute-start(bf16[192,256]{1,0:T(8,128)(2,1)S(1)} %pad_maximum_fusion.refs_0_), channel_id=1, source_target_pairs={{0,4},{1,5},{2,6},{3,7},{4,0},{5,1},{6,2},{7,3},{8,12},{9,13},{10,... | collective-permute-start | bytes 294920 | tf_op jit(solution)/shard_map/ppermute | solution.py:233
  3.9 3.6 %collective-permute-start.4 = (bf16[192,256]{1,0:T(8,128)(2,1)S(1)}, bf16[192,256]{1,0:T(8,128)(2,1)S(1)}, u32[]{:S(2)}, u32[]{:S(2)}) collective-permute-start(bf16[192,256]{1,0:T(8,128)(2,1)S(1)} %pad_maximum_fusion.refs_0_), channel_id=1, source_target_pairs={{0,24},{1,13},{2,26},{3,15},{4,28},{5,9},{6,30},{7,11},{8,16},{9,5... | collective-permute-start | bytes 294920 | tf_op jit(solution)/shard_map/ppermute | solution.py:233
  7.5 0.0 collective-permute-start.3
  7.5 0.8 %collective-permute-start.2 = (bf16[192,256]{1,0:T(8,128)(2,1)S(1)}, bf16[192,256]{1,0:T(8,128)(2,1)S(1)}, u32[]{:S(2)}, u32[]{:S(2)}) collective-permute-start(bf16[192,256]{1,0:T(8,128)(2,1)S(1)} %pad_maximum_fusion.refs_0_), channel_id=1, source_target_pairs={{0,16},{1,21},{2,18},{3,23},{4,20},{5,17},{6,22},{7,19},{8,24},{9,... | collective-permute-start | bytes 294920 | tf_op jit(solution)/shard_map/ppermute | solution.py:233
  8.3 0.0 copy-start
  8.3 0.7 %copy-done = s32[1536]{0:T(1024)S(1)} copy-done((s32[1536]{0:T(1024)S(1)}, s32[1536]{0:T(1024)}, u32[]{:S(2)}) %copy-start) | copy-done | bytes 6168
  9.0 2.6 %prepare.1 = (f32[96,1536]{1,0:T(8,128)S(1)}, bf16[96,512]{1,0:T(8,128)(2,1)S(1)}, bf16[96,512]{1,0:T(8,128)(2,1)S(1)}, bf16[512,2560]{1,0:T(8,128)(2,1)S(1)}) custom-call(s32[1536]{0:T(1024)S(1)} %copy-done, bf16[192,512]{1,0:T(8,128)(2,1)} %queries_ref.1, bf16[512,8192]{1,0:T(8,128)(2,1)} %own_w_ref.7), custom_call_target="tpu_custom_call" | custom-call | tf_op jit(solution)/shard_map/prepare/pallas_call | solution.py:268
  11.5 0.0 collective-permute-done.5.refs_4_
  11.5 0.4 collective-permute-start.1
  12.0 0.0 collective-permute-done.4.refs_3_
  12.0 0.2 collective-permute-start.8
  12.1 1.2 %collective-permute-done.3.refs_2_ = bf16[192,256]{1,0:T(8,128)(2,1)S(1)} collective-permute-done((bf16[192,256]{1,0:T(8,128)(2,1)S(1)}, bf16[192,256]{1,0:T(8,128)(2,1)S(1)}, u32[]{:S(2)}, u32[]{:S(2)}) %collective-permute-start.3) | collective-permute-done | bytes 98336 | tf_op jit(solution)/shard_map/ppermute | solution.py:233
  13.3 0.0 collective-permute-start.7
  13.3 3.3 %collective-permute-done.2.refs_1_ = bf16[192,256]{1,0:T(8,128)(2,1)S(1)} collective-permute-done((bf16[192,256]{1,0:T(8,128)(2,1)S(1)}, bf16[192,256]{1,0:T(8,128)(2,1)S(1)}, u32[]{:S(2)}, u32[]{:S(2)}) %collective-permute-start.2) | collective-permute-done | bytes 98336 | tf_op jit(solution)/shard_map/ppermute | solution.py:233
  16.6 0.4 collective-permute-start.6
  17.0 0.0 collective-permute-done.1.sib_ref
  17.0 0.0 collective-permute-done.8.refs_7_
  17.0 0.0 collective-permute-done.7.refs_6_
  17.0 0.9 %collective-permute-done.6.refs_5_ = bf16[192,256]{1,0:T(8,128)(2,1)S(1)} collective-permute-done((bf16[192,256]{1,0:T(8,128)(2,1)S(1)}, bf16[192,256]{1,0:T(8,128)(2,1)S(1)}, u32[]{:S(2)}, u32[]{:S(2)}) %collective-permute-start.6) | collective-permute-done | bytes 98336 | tf_op jit(solution)/shard_map/ppermute | solution.py:233
  17.9 0.0 collective-permute-done.sib_w_ref
  17.9 1.8 %send.1 = (bf16[48,1024]{1,0:T(8,128)(2,1)S(1)}, bf16[48,1024]{1,0:T(8,128)(2,1)S(1)}, bf16[512,2560]{1,0:T(8,128)(2,1)S(1)}) custom-call(f32[96,1536]{1,0:T(8,128)S(1)} %get-tuple-element.21.bias_ref, bf16[96,512]{1,0:T(8,128)(2,1)S(1)} %get-tuple-element.22.own_ref, bf16[96,512]{1,0:T(8,128)(2,1)S(1)} %collective-permute-done.1.sib_ref, ...), custom_call_target="tpu_custom_call" | custom-call | tf_op jit(solution)/shard_map/send/pallas_call | solution.py:304
  19.7 2.6 %shard_map.55 = (bf16[48,1024]{1,0:T(8,128)(2,1)S(1)}, bf16[48,2048]{1,0:T(8,128)(2,1)S(1)}, bf16[48,2048]{1,0:T(8,128)(2,1)S(1)}) custom-call(f32[96,1536]{1,0:T(8,128)S(1)} %get-tuple-element.21.bias_ref, bf16[96,512]{1,0:T(8,128)(2,1)S(1)} %get-tuple-element.22.own_ref, bf16[96,512]{1,0:T(8,128)(2,1)S(1)} %collective-permute-done.1.sib_ref, ...), custom_call_target="tpu_custom_call" | custom-call | tf_op jit(solution)/shard_map/pallas_call | solution.py:286
  22.2 1.6 %collective-permute-start.11 = (bf16[48,2048]{1,0:T(8,128)(2,1)S(1)}, bf16[48,2048]{1,0:T(8,128)(2,1)S(1)}, u32[]{:S(2)}, u32[]{:S(2)}) collective-permute-start(bf16[48,2048]{1,0:T(8,128)(2,1)S(1)} %get-tuple-element.32), channel_id=1, source_target_pairs={{0,2},{1,3},{2,0},{3,1},{4,6},{5,7},{6,4},{7,5},{8,10},{9,11},{10,... | collective-permute-start | bytes 589832 | tf_op jit(solution)/shard_map/ppermute | solution.py:233
  23.8 2.6 %shard_map.57 = (bf16[48,2048]{1,0:T(8,128)(2,1)S(1)}, bf16[48,2048]{1,0:T(8,128)(2,1)S(1)}) custom-call(bf16[512,8192]{1,0:T(8,128)(2,1)} %own_w_ref.7, bf16[512,8192]{1,0:T(8,128)(2,1)} %collective-permute-done.sib_w_ref, bf16[48,1024]{1,0:T(8,128)(2,1)S(1)} %get-tuple-element.26.refs_0_.attended_ref, ...), custom_call_target="tpu_custom_call" | custom-call | tf_op jit(solution)/shard_map/pallas_call | solution.py:286
  26.4 0.6 %collective-permute-start.10 = (bf16[48,2048]{1,0:T(8,128)(2,1)S(1)}, bf16[48,2048]{1,0:T(8,128)(2,1)S(1)}, u32[]{:S(2)}, u32[]{:S(2)}) collective-permute-start(bf16[48,2048]{1,0:T(8,128)(2,1)S(1)} %get-tuple-element.30), channel_id=1, source_target_pairs={{0,2},{1,3},{2,0},{3,1},{4,6},{5,7},{6,4},{7,5},{8,10},{9,11},{10,... | collective-permute-start | bytes 589832 | tf_op jit(solution)/shard_map/ppermute | solution.py:233
  26.9 0.6 %again.1 = bf16[48,1536]{1,0:T(8,128)(2,1)S(1)} custom-call(bf16[48,1024]{1,0:T(8,128)(2,1)S(1)} %get-tuple-element.25.sent_ref.refs_1_.attended_ref, bf16[512,2560]{1,0:T(8,128)(2,1)S(1)} %get-tuple-element.24.own_part_ref, bf16[512,2560]{1,0:T(8,128)(2,1)S(1)} %get-tuple-element.33.sib_part_ref), custom_call_target="tpu_custom_call" | custom-call | tf_op jit(solution)/shard_map/again/pallas_call | solution.py:314
  27.6 1.6 %collective-permute-start.12 = (bf16[48,1536]{1,0:T(8,128)(2,1)S(1)}, bf16[48,1536]{1,0:T(8,128)(2,1)S(1)}, u32[]{:S(2)}, u32[]{:S(2)}) collective-permute-start(bf16[48,1536]{1,0:T(8,128)(2,1)S(1)} %again.1), channel_id=1, source_target_pairs={{0,2},{1,3},{2,0},{3,1},{4,6},{5,7},{6,4},{7,5},{8,10},{9,11},{10,... | collective-permute-start | bytes 442376 | tf_op jit(solution)/shard_map/ppermute | solution.py:233
  29.2 2.2 %shard_map.56 = (bf16[48,1536]{1,0:T(8,128)(2,1)S(1)}, bf16[48,1536]{1,0:T(8,128)(2,1)S(1)}) custom-call(bf16[512,8192]{1,0:T(8,128)(2,1)} %own_w_ref.7, bf16[512,8192]{1,0:T(8,128)(2,1)} %collective-permute-done.sib_w_ref, bf16[48,1024]{1,0:T(8,128)(2,1)S(1)} %get-tuple-element.26.refs_0_.attended_ref, ...), custom_call_target="tpu_custom_call" | custom-call | tf_op jit(solution)/shard_map/pallas_call | solution.py:286
  31.4 0.6 %collective-permute-start.9 = (bf16[48,1536]{1,0:T(8,128)(2,1)S(1)}, bf16[48,1536]{1,0:T(8,128)(2,1)S(1)}, u32[]{:S(2)}, u32[]{:S(2)}) collective-permute-start(bf16[48,1536]{1,0:T(8,128)(2,1)S(1)} %get-tuple-element.28), channel_id=1, source_target_pairs={{0,2},{1,3},{2,0},{3,1},{4,6},{5,7},{6,4},{7,5},{8,10},{9,11},{10,... | collective-permute-start | bytes 442376 | tf_op jit(solution)/shard_map/ppermute | solution.py:233
  32.0 1.5 %collective-permute-start.13 = (bf16[48,1024]{1,0:T(8,128)(2,1)S(1)}, bf16[48,1024]{1,0:T(8,128)(2,1)S(1)}, u32[]{:S(2)}, u32[]{:S(2)}) collective-permute-start(bf16[48,1024]{1,0:T(8,128)(2,1)S(1)} %get-tuple-element.36), channel_id=1, source_target_pairs={{0,2},{1,3},{2,0},{3,1},{4,6},{5,7},{6,4},{7,5},{8,10},{9,11},{10,... | collective-permute-start | bytes 294920 | tf_op jit(solution)/shard_map/ppermute | solution.py:233
  33.5 1.0 %rest.1 = (bf16[48,1024]{1,0:T(8,128)(2,1)S(1)}, bf16[48,1536]{1,0:T(8,128)(2,1)S(1)}) custom-call(bf16[48,1024]{1,0:T(8,128)(2,1)S(1)} %get-tuple-element.26.refs_0_.attended_ref, bf16[512,2560]{1,0:T(8,128)(2,1)S(1)} %get-tuple-element.24.own_part_ref, bf16[512,2560]{1,0:T(8,128)(2,1)S(1)} %get-tuple-element.33.sib_part_ref), custom_call_target="tpu_custom_call" | custom-call | tf_op jit(solution)/shard_map/rest/pallas_call | solution.py:340
  34.5 7.6 %collective-permute-done.13.refs_1_ = bf16[48,1024]{1,0:T(8,128)(2,1)S(1)} collective-permute-done((bf16[48,1024]{1,0:T(8,128)(2,1)S(1)}, bf16[48,1024]{1,0:T(8,128)(2,1)S(1)}, u32[]{:S(2)}, u32[]{:S(2)}) %collective-permute-start.13) | collective-permute-done | bytes 98336 | tf_op jit(solution)/shard_map/ppermute | solution.py:233
  42.1 0.7 %finish.5.refs_2_ = bf16[48,8192]{1,0:T(8,128)(2,1)} custom-call(bf16[48,1024]{1,0:T(8,128)(2,1)S(1)} %get-tuple-element.35.refs_0_, bf16[48,1024]{1,0:T(8,128)(2,1)S(1)} %collective-permute-done.13.refs_1_), custom_call_target="tpu_custom_call" | custom-call | tf_op jit(solution)/shard_map/finish/pallas_call | solution.py:349
  42.8 0.0 collective-permute-done.12.refs_1_
  42.8 0.7 %finish.6.refs_2_ = bf16[48,8192]{1,0:T(8,128)(2,1)} custom-call(bf16[48,1536]{1,0:T(8,128)(2,1)S(1)} %get-tuple-element.34.refs_0_, bf16[48,1536]{1,0:T(8,128)(2,1)S(1)} %collective-permute-done.12.refs_1_, bf16[48,8192]{1,0:T(8,128)(2,1)} %finish.5.refs_2_), custom_call_target="tpu_custom_call", output_to_operand_aliasing={{}: (2, {})} | custom-call | tf_op jit(solution)/shard_map/finish/pallas_call | solution.py:349
  43.5 0.0 collective-permute-done.11.refs_1_
  43.5 0.7 %finish.7.refs_2_ = bf16[48,8192]{1,0:T(8,128)(2,1)} custom-call(bf16[48,2048]{1,0:T(8,128)(2,1)S(1)} %get-tuple-element.31.refs_0_, bf16[48,2048]{1,0:T(8,128)(2,1)S(1)} %collective-permute-done.11.refs_1_, bf16[48,8192]{1,0:T(8,128)(2,1)} %finish.6.refs_2_), custom_call_target="tpu_custom_call", output_to_operand_aliasing={{}: (2, {})} | custom-call | tf_op jit(solution)/shard_map/finish/pallas_call | solution.py:349
  44.3 0.0 collective-permute-done.10.refs_1_
  44.3 0.7 %finish.8.refs_2_ = bf16[48,8192]{1,0:T(8,128)(2,1)} custom-call(bf16[48,2048]{1,0:T(8,128)(2,1)S(1)} %get-tuple-element.29.refs_0_, bf16[48,2048]{1,0:T(8,128)(2,1)S(1)} %collective-permute-done.10.refs_1_, bf16[48,8192]{1,0:T(8,128)(2,1)} %finish.7.refs_2_), custom_call_target="tpu_custom_call", output_to_operand_aliasing={{}: (2, {})} | custom-call | tf_op jit(solution)/shard_map/finish/pallas_call | solution.py:349
  45.0 0.0 collective-permute-done.9.refs_1_
  45.0 0.7 %finish.9 = bf16[48,8192]{1,0:T(8,128)(2,1)} custom-call(bf16[48,1536]{1,0:T(8,128)(2,1)S(1)} %get-tuple-element.27.refs_0_, bf16[48,1536]{1,0:T(8,128)(2,1)S(1)} %collective-permute-done.9.refs_1_, bf16[48,8192]{1,0:T(8,128)(2,1)} %finish.8.refs_2_), custom_call_target="tpu_custom_call", output_to_operand_aliasing={{}: (2, {})} | custom-call | tf_op jit(solution)/shard_map/finish/pallas_call | solution.py:349
  (1 shorter events, 0.0 us)
Async XLA Ops:
  0.0 17.9 %collective-permute-start = (bf16[512,8192]{1,0:T(8,128)(2,1)}, bf16[512,8192]{1,0:T(8,128)(2,1)}, u32[]{:S(2)}, u32[]{:S(2)}) collective-permute-start(bf16[512,8192]{1,0:T(8,128)(2,1)} %own_w_ref.7), channel_id=1, source_target_pairs={{0,1},{1,0},{2,3},{3,2},{4,5},{5,4},{6,7},{7,6},{8,9},{9,8},{10,11... | collective-permute-start | bytes 25165832 | tf_op jit(solution)/shard_map/ppermute | solution.py:233
  1.3 10.2 %collective-permute-start.5 = (bf16[192,256]{1,0:T(8,128)(2,1)S(1)}, bf16[192,256]{1,0:T(8,128)(2,1)S(1)}, u32[]{:S(2)}, u32[]{:S(2)}) collective-permute-start(bf16[192,256]{1,0:T(8,128)(2,1)S(1)} %pad_maximum_fusion.refs_0_), channel_id=1, source_target_pairs={{0,4},{1,5},{2,6},{3,7},{4,0},{5,1},{6,2},{7,3},{8,12},{9,13},{10,... | collective-permute-start | bytes 294920 | tf_op jit(solution)/shard_map/ppermute | solution.py:233
  3.9 8.1 %collective-permute-start.4 = (bf16[192,256]{1,0:T(8,128)(2,1)S(1)}, bf16[192,256]{1,0:T(8,128)(2,1)S(1)}, u32[]{:S(2)}, u32[]{:S(2)}) collective-permute-start(bf16[192,256]{1,0:T(8,128)(2,1)S(1)} %pad_maximum_fusion.refs_0_), channel_id=1, source_target_pairs={{0,24},{1,13},{2,26},{3,15},{4,28},{5,9},{6,30},{7,11},{8,16},{9,5... | collective-permute-start | bytes 294920 | tf_op jit(solution)/shard_map/ppermute | solution.py:233
  7.5 5.8 %collective-permute-start.3 = (bf16[192,256]{1,0:T(8,128)(2,1)S(1)}, bf16[192,256]{1,0:T(8,128)(2,1)S(1)}, u32[]{:S(2)}, u32[]{:S(2)}) collective-permute-start(bf16[192,256]{1,0:T(8,128)(2,1)S(1)} %pad_maximum_fusion.refs_0_), channel_id=1, source_target_pairs={{0,8},{1,29},{2,10},{3,31},{4,12},{5,25},{6,14},{7,27},{8,0},{9,21... | collective-permute-start | bytes 294920 | tf_op jit(solution)/shard_map/ppermute | solution.py:233
  7.5 9.1 %collective-permute-start.2 = (bf16[192,256]{1,0:T(8,128)(2,1)S(1)}, bf16[192,256]{1,0:T(8,128)(2,1)S(1)}, u32[]{:S(2)}, u32[]{:S(2)}) collective-permute-start(bf16[192,256]{1,0:T(8,128)(2,1)S(1)} %pad_maximum_fusion.refs_0_), channel_id=1, source_target_pairs={{0,16},{1,21},{2,18},{3,23},{4,20},{5,17},{6,22},{7,19},{8,24},{9,... | collective-permute-start | bytes 294920 | tf_op jit(solution)/shard_map/ppermute | solution.py:233
  8.3 0.7 %copy-start = (s32[1536]{0:T(1024)S(1)}, s32[1536]{0:T(1024)}, u32[]{:S(2)}) copy-start(s32[1536]{0:T(1024)} %positions_ref.1) | copy-start | bytes 18436
  11.5 5.4 %collective-permute-start.1 = (bf16[96,512]{1,0:T(8,128)(2,1)S(1)}, bf16[96,512]{1,0:T(8,128)(2,1)S(1)}, u32[]{:S(2)}, u32[]{:S(2)}) collective-permute-start(bf16[96,512]{1,0:T(8,128)(2,1)S(1)} %get-tuple-element.23), channel_id=1, source_target_pairs={{0,1},{1,0},{2,3},{3,2},{4,5},{5,4},{6,7},{7,6},{8,9},{9,8},{10,11... | collective-permute-start | bytes 294920 | tf_op jit(solution)/shard_map/ppermute | solution.py:233
  12.0 5.0 %collective-permute-start.8 = (bf16[192,256]{1,0:T(8,128)(2,1)S(1)}, bf16[192,256]{1,0:T(8,128)(2,1)S(1)}, u32[]{:S(2)}, u32[]{:S(2)}) collective-permute-start(bf16[192,256]{1,0:T(8,128)(2,1)S(1)} %collective-permute-done.4.refs_3_), channel_id=1, source_target_pairs={{0,1},{1,0},{2,3},{3,2},{4,5},{5,4},{6,7},{7,6},{8,9},{9,8},{10,11... | collective-permute-start | bytes 294920 | tf_op jit(solution)/shard_map/ppermute | solution.py:233
  13.3 3.7 %collective-permute-start.7 = (bf16[192,256]{1,0:T(8,128)(2,1)S(1)}, bf16[192,256]{1,0:T(8,128)(2,1)S(1)}, u32[]{:S(2)}, u32[]{:S(2)}) collective-permute-start(bf16[192,256]{1,0:T(8,128)(2,1)S(1)} %collective-permute-done.3.refs_2_), channel_id=1, source_target_pairs={{0,1},{1,0},{2,3},{3,2},{4,5},{5,4},{6,7},{7,6},{8,9},{9,8},{10,11... | collective-permute-start | bytes 294920 | tf_op jit(solution)/shard_map/ppermute | solution.py:233
  16.6 1.3 %collective-permute-start.6 = (bf16[192,256]{1,0:T(8,128)(2,1)S(1)}, bf16[192,256]{1,0:T(8,128)(2,1)S(1)}, u32[]{:S(2)}, u32[]{:S(2)}) collective-permute-start(bf16[192,256]{1,0:T(8,128)(2,1)S(1)} %collective-permute-done.2.refs_1_), channel_id=1, source_target_pairs={{0,1},{1,0},{2,3},{3,2},{4,5},{5,4},{6,7},{7,6},{8,9},{9,8},{10,11... | collective-permute-start | bytes 294920 | tf_op jit(solution)/shard_map/ppermute | solution.py:233
  22.2 21.3 %collective-permute-start.11 = (bf16[48,2048]{1,0:T(8,128)(2,1)S(1)}, bf16[48,2048]{1,0:T(8,128)(2,1)S(1)}, u32[]{:S(2)}, u32[]{:S(2)}) collective-permute-start(bf16[48,2048]{1,0:T(8,128)(2,1)S(1)} %get-tuple-element.32), channel_id=1, source_target_pairs={{0,2},{1,3},{2,0},{3,1},{4,6},{5,7},{6,4},{7,5},{8,10},{9,11},{10,... | collective-permute-start | bytes 589832 | tf_op jit(solution)/shard_map/ppermute | solution.py:233
  26.4 17.9 %collective-permute-start.10 = (bf16[48,2048]{1,0:T(8,128)(2,1)S(1)}, bf16[48,2048]{1,0:T(8,128)(2,1)S(1)}, u32[]{:S(2)}, u32[]{:S(2)}) collective-permute-start(bf16[48,2048]{1,0:T(8,128)(2,1)S(1)} %get-tuple-element.30), channel_id=1, source_target_pairs={{0,2},{1,3},{2,0},{3,1},{4,6},{5,7},{6,4},{7,5},{8,10},{9,11},{10,... | collective-permute-start | bytes 589832 | tf_op jit(solution)/shard_map/ppermute | solution.py:233
  27.6 15.2 %collective-permute-start.12 = (bf16[48,1536]{1,0:T(8,128)(2,1)S(1)}, bf16[48,1536]{1,0:T(8,128)(2,1)S(1)}, u32[]{:S(2)}, u32[]{:S(2)}) collective-permute-start(bf16[48,1536]{1,0:T(8,128)(2,1)S(1)} %again.1), channel_id=1, source_target_pairs={{0,2},{1,3},{2,0},{3,1},{4,6},{5,7},{6,4},{7,5},{8,10},{9,11},{10,... | collective-permute-start | bytes 442376 | tf_op jit(solution)/shard_map/ppermute | solution.py:233
  31.4 13.6 %collective-permute-start.9 = (bf16[48,1536]{1,0:T(8,128)(2,1)S(1)}, bf16[48,1536]{1,0:T(8,128)(2,1)S(1)}, u32[]{:S(2)}, u32[]{:S(2)}) collective-permute-start(bf16[48,1536]{1,0:T(8,128)(2,1)S(1)} %get-tuple-element.28), channel_id=1, source_target_pairs={{0,2},{1,3},{2,0},{3,1},{4,6},{5,7},{6,4},{7,5},{8,10},{9,11},{10,... | collective-permute-start | bytes 442376 | tf_op jit(solution)/shard_map/ppermute | solution.py:233
  32.0 10.1 %collective-permute-start.13 = (bf16[48,1024]{1,0:T(8,128)(2,1)S(1)}, bf16[48,1024]{1,0:T(8,128)(2,1)S(1)}, u32[]{:S(2)}, u32[]{:S(2)}) collective-permute-start(bf16[48,1024]{1,0:T(8,128)(2,1)S(1)} %get-tuple-element.36), channel_id=1, source_target_pairs={{0,2},{1,3},{2,0},{3,1},{4,6},{5,7},{6,4},{7,5},{8,10},{9,11},{10,... | collective-permute-start | bytes 294920 | tf_op jit(solution)/shard_map/ppermute | solution.py:233

commit v4 on v3

--- a/solution.py
+++ b/solution.py
@@ -90,8 +90,10 @@
             at += ref.shape[0]
 
 
-def prepare_kernel(offsets, positions_ref, queries_ref, own_w_ref, *refs):
-    bias_ref, own_ref, swap_ref, weight_ref, sems = refs
+def prepare_kernel(offsets, all_positions_ref, queries_ref, own_w_ref, *refs):
+    bias_ref, own_ref, swap_ref, weight_ref, positions_ref, sems = refs
+    positions_load = pltpu.make_async_copy(all_positions_ref, positions_ref, sems.at[5])
+    positions_load.start()
     rows = queries_ref.shape[0]
     part = own_ref.shape[0] // 2
     run = rows // 2
@@ -114,6 +116,7 @@
             )
     for load in loads[1:] + loads[:1]:
         load.start()
+    positions_load.wait()
     lane = lax.broadcasted_iota(jnp.int32, (1, bias_ref.shape[1]), 1)
     key_pos = lane
     for j, (a, b) in enumerate(offsets):
@@ -267,17 +270,20 @@
     mine = (2 * part, heads * HEAD)
     bias, own_q, swap_q, own_part = pl.pallas_call(
         functools.partial(prepare_kernel, offsets),
-        in_specs=[pl.BlockSpec(memory_space=pltpu.SMEM), hbm, hbm],
+        in_specs=[hbm, hbm, hbm],
         out_shape=(
             pltpu.VMEM((2 * part, token_count), jnp.float32),
             pltpu.VMEM(mine, jnp.bfloat16),
             pltpu.VMEM(mine, jnp.bfloat16),
             pltpu.VMEM((heads * HEAD, cuts[2]), jnp.bfloat16),
         ),
-        scratch_shapes=[pltpu.SemaphoreType.DMA((5,))],
+        scratch_shapes=[
+            pltpu.SMEM((token_count,), jnp.int32),
+            pltpu.SemaphoreType.DMA((6,)),
+        ],
         compiler_params=pltpu.CompilerParams(vmem_limit_bytes=VMEM_LIMIT),
         name="prepare",
-    )(positions, pltpu.with_memory_space_constraint(queries, pltpu.HBM), weights[0])
+    )(*[pltpu.with_memory_space_constraint(x, pltpu.HBM) for x in (positions, queries)], weights[0])
     sib_q = to_sibling(swap_q)
     inputs = [vmem(bias), vmem(own_q), vmem(sib_q)]
     kv = [vmem(b) for b in blocks]

time: 46.1 us -> 46 us (level)
  waiting for transfers between devices: 13 us -> 14.5 us
  local copies, waits for them, and re-layouts: 1.53 us -> 0.83 us
  Pallas kernels: 16.8 us -> 16.2 us
    ppermute x14, waiting for transfers between devices: 13 us -> 14.5 us  [permute(): return lax.ppermute(x, AXES, pairs)]
    unnamed x2 -> x0, local copies, waits for them, and re-layouts: 0.7 us -> none
    pallas_call x1, Pallas kernels: 2.56 us -> 1.91 us  [shards(): pl.pallas_call(functools.partial(prepare_kernel, offsets), in_specs=[hbm,...]
  transfers between devices with their start and end apart: 14 -> 14, of which waited for: 4 -> 5; matrix products, arithmetic and copies ran while one was open for 2% -> 2% of each run, Pallas kernels for 26% -> 24%
where the time goes in v4:
time: 46 us; the launch traced here: 45.8 us
  Pallas kernels  16.2 us (35%)
  waiting for transfers between devices  14.5 us (32%)
  starting transfers between devices  14 us (30%)
  local copies, waits for them, and re-layouts  0.83 us (2%)
    ppermute x14, waiting for transfers between devices, permute(): return lax.ppermute(x, AXES, pairs)  14.5 us
    ppermute x14, starting transfers between devices, permute(): return lax.ppermute(x, AXES, pairs)  14 us
    pallas_call x3, Pallas kernels, call(): pl.pallas_call(kernel, in_specs=in_specs, out_shape=out_shape, scratch_sh...  7.36 us
    pallas_call x5, Pallas kernels, shards(): pl.pallas_call(functools.partial(finish_kernel, lo), in_specs=[whole, who...  3.56 us
    pallas_call x1, Pallas kernels, shards(): pl.pallas_call(functools.partial(prepare_kernel, offsets), in_specs=[hbm,...  1.91 us
    pallas_call x1, Pallas kernels, shards(): pl.pallas_call(functools.partial(send_kernel, stack), in_specs=[whole] *...  1.75 us
    pallas_call x1, Pallas kernels, shards(): pl.pallas_call(functools.partial(resident_kernel, 0), in_specs=[whole] *...  0.99 us
  transfers between devices with their start and end apart: 14, of which 5 were waited for; matrix products, arithmetic and copies ran while one was open for 2% of the time, Pallas kernels for 24%

profile of v4, /device:TPU:0, one launch (start us, length us, event | category | flops | bytes accessed | tf_op | source)
XLA Modules:
  0.0 45.8 jit_solution(13874077239450986062)
XLA Ops:
  0.0 0.5 %collective-permute-start = (bf16[512,8192]{1,0:T(8,128)(2,1)}, bf16[512,8192]{1,0:T(8,128)(2,1)}, u32[]{:S(2)}, u32[]{:S(2)}) collective-permute-start(bf16[512,8192]{1,0:T(8,128)(2,1)} %own_w_ref.7), channel_id=1, source_target_pairs={{0,1},{1,0},{2,3},{3,2},{4,5},{5,4},{6,7},{7,6},{8,9},{9,8},{10,11... | collective-permute-start | bytes 25165832 | tf_op jit(solution)/shard_map/ppermute | solution.py:236
  0.5 0.8 %constant_dynamic-slice_fusion = (bf16[192,128]{1,0:T(8,128)(2,1)S(1)}, bf16[192,128]{1,0:T(8,128)(2,1)S(1)}) fusion(bf16[192,256]{1,0:T(8,128)(2,1)} %param.7, s32[]{:T(128)S(6)} %select_n.10, bf16[192,256]{1,0:T(8,128)(2,1)} %param.6), kind=kLoop, calls=%fused_computation.1 | loop fusion | bytes 196612 | tf_op jit(solution)/shard_map/dynamic_slice | solution.py:243
  1.3 2.5 %collective-permute-start.5 = (bf16[192,256]{1,0:T(8,128)(2,1)S(1)}, bf16[192,256]{1,0:T(8,128)(2,1)S(1)}, u32[]{:S(2)}, u32[]{:S(2)}) collective-permute-start(bf16[192,256]{1,0:T(8,128)(2,1)S(1)} %pad_maximum_fusion.refs_0_), channel_id=1, source_target_pairs={{0,4},{1,5},{2,6},{3,7},{4,0},{5,1},{6,2},{7,3},{8,12},{9,13},{10,... | collective-permute-start | bytes 294920 | tf_op jit(solution)/shard_map/ppermute | solution.py:236
  3.9 3.6 %collective-permute-start.4 = (bf16[192,256]{1,0:T(8,128)(2,1)S(1)}, bf16[192,256]{1,0:T(8,128)(2,1)S(1)}, u32[]{:S(2)}, u32[]{:S(2)}) collective-permute-start(bf16[192,256]{1,0:T(8,128)(2,1)S(1)} %pad_maximum_fusion.refs_0_), channel_id=1, source_target_pairs={{0,24},{1,13},{2,26},{3,15},{4,28},{5,9},{6,30},{7,11},{8,16},{9,5... | collective-permute-start | bytes 294920 | tf_op jit(solution)/shard_map/ppermute | solution.py:236
  7.5 0.0 collective-permute-start.3
  7.5 0.8 %collective-permute-start.2 = (bf16[192,256]{1,0:T(8,128)(2,1)S(1)}, bf16[192,256]{1,0:T(8,128)(2,1)S(1)}, u32[]{:S(2)}, u32[]{:S(2)}) collective-permute-start(bf16[192,256]{1,0:T(8,128)(2,1)S(1)} %pad_maximum_fusion.refs_0_), channel_id=1, source_target_pairs={{0,16},{1,21},{2,18},{3,23},{4,20},{5,17},{6,22},{7,19},{8,24},{9,... | collective-permute-start | bytes 294920 | tf_op jit(solution)/shard_map/ppermute | solution.py:236
  8.3 1.9 %prepare.1 = (f32[96,1536]{1,0:T(8,128)S(1)}, bf16[96,512]{1,0:T(8,128)(2,1)S(1)}, bf16[96,512]{1,0:T(8,128)(2,1)S(1)}, bf16[512,2560]{1,0:T(8,128)(2,1)S(1)}) custom-call(s32[1536]{0:T(1024)} %all_positions_ref.1, bf16[192,512]{1,0:T(8,128)(2,1)} %queries_ref.1, bf16[512,8192]{1,0:T(8,128)(2,1)} %own_w_ref.7), custom_call_target="tpu_custom_call" | custom-call | tf_op jit(solution)/shard_map/prepare/pallas_call | solution.py:271
  10.2 0.0 collective-permute-done.5.refs_4_
  10.2 0.4 collective-permute-start.1
  10.6 0.4 collective-permute-done.4.refs_3_
  11.0 0.0 collective-permute-start.8
  11.0 2.3 %collective-permute-done.3.refs_2_ = bf16[192,256]{1,0:T(8,128)(2,1)S(1)} collective-permute-done((bf16[192,256]{1,0:T(8,128)(2,1)S(1)}, bf16[192,256]{1,0:T(8,128)(2,1)S(1)}, u32[]{:S(2)}, u32[]{:S(2)}) %collective-permute-start.3) | collective-permute-done | bytes 98336 | tf_op jit(solution)/shard_map/ppermute | solution.py:236
  13.3 0.0 collective-permute-start.7
  13.3 3.3 %collective-permute-done.2.refs_1_ = bf16[192,256]{1,0:T(8,128)(2,1)S(1)} collective-permute-done((bf16[192,256]{1,0:T(8,128)(2,1)S(1)}, bf16[192,256]{1,0:T(8,128)(2,1)S(1)}, u32[]{:S(2)}, u32[]{:S(2)}) %collective-permute-start.2) | collective-permute-done | bytes 98336 | tf_op jit(solution)/shard_map/ppermute | solution.py:236
  16.6 0.4 collective-permute-start.6
  17.0 0.0 collective-permute-done.1.sib_ref
  17.0 0.0 collective-permute-done.8.refs_7_
  17.0 0.0 collective-permute-done.7.refs_6_
  17.0 0.9 %collective-permute-done.6.refs_5_ = bf16[192,256]{1,0:T(8,128)(2,1)S(1)} collective-permute-done((bf16[192,256]{1,0:T(8,128)(2,1)S(1)}, bf16[192,256]{1,0:T(8,128)(2,1)S(1)}, u32[]{:S(2)}, u32[]{:S(2)}) %collective-permute-start.6) | collective-permute-done | bytes 98336 | tf_op jit(solution)/shard_map/ppermute | solution.py:236
  17.9 0.0 collective-permute-done.sib_w_ref
  17.9 1.8 %send.1 = (bf16[48,1024]{1,0:T(8,128)(2,1)S(1)}, bf16[48,1024]{1,0:T(8,128)(2,1)S(1)}, bf16[512,2560]{1,0:T(8,128)(2,1)S(1)}) custom-call(f32[96,1536]{1,0:T(8,128)S(1)} %get-tuple-element.21.bias_ref, bf16[96,512]{1,0:T(8,128)(2,1)S(1)} %get-tuple-element.22.own_ref, bf16[96,512]{1,0:T(8,128)(2,1)S(1)} %collective-permute-done.1.sib_ref, ...), custom_call_target="tpu_custom_call" | custom-call | tf_op jit(solution)/shard_map/send/pallas_call | solution.py:310
  19.7 2.6 %shard_map.55 = (bf16[48,1024]{1,0:T(8,128)(2,1)S(1)}, bf16[48,2048]{1,0:T(8,128)(2,1)S(1)}, bf16[48,2048]{1,0:T(8,128)(2,1)S(1)}) custom-call(f32[96,1536]{1,0:T(8,128)S(1)} %get-tuple-element.21.bias_ref, bf16[96,512]{1,0:T(8,128)(2,1)S(1)} %get-tuple-element.22.own_ref, bf16[96,512]{1,0:T(8,128)(2,1)S(1)} %collective-permute-done.1.sib_ref, ...), custom_call_target="tpu_custom_call" | custom-call | tf_op jit(solution)/shard_map/pallas_call | solution.py:292
  22.3 1.6 %collective-permute-start.11 = (bf16[48,2048]{1,0:T(8,128)(2,1)S(1)}, bf16[48,2048]{1,0:T(8,128)(2,1)S(1)}, u32[]{:S(2)}, u32[]{:S(2)}) collective-permute-start(bf16[48,2048]{1,0:T(8,128)(2,1)S(1)} %get-tuple-element.32), channel_id=1, source_target_pairs={{0,2},{1,3},{2,0},{3,1},{4,6},{5,7},{6,4},{7,5},{8,10},{9,11},{10,... | collective-permute-start | bytes 589832 | tf_op jit(solution)/shard_map/ppermute | solution.py:236
  23.9 2.6 %shard_map.57 = (bf16[48,2048]{1,0:T(8,128)(2,1)S(1)}, bf16[48,2048]{1,0:T(8,128)(2,1)S(1)}) custom-call(bf16[512,8192]{1,0:T(8,128)(2,1)} %own_w_ref.7, bf16[512,8192]{1,0:T(8,128)(2,1)} %collective-permute-done.sib_w_ref, bf16[48,1024]{1,0:T(8,128)(2,1)S(1)} %get-tuple-element.26.refs_0_.attended_ref, ...), custom_call_target="tpu_custom_call" | custom-call | tf_op jit(solution)/shard_map/pallas_call | solution.py:292
  26.4 0.6 %collective-permute-start.10 = (bf16[48,2048]{1,0:T(8,128)(2,1)S(1)}, bf16[48,2048]{1,0:T(8,128)(2,1)S(1)}, u32[]{:S(2)}, u32[]{:S(2)}) collective-permute-start(bf16[48,2048]{1,0:T(8,128)(2,1)S(1)} %get-tuple-element.30), channel_id=1, source_target_pairs={{0,2},{1,3},{2,0},{3,1},{4,6},{5,7},{6,4},{7,5},{8,10},{9,11},{10,... | collective-permute-start | bytes 589832 | tf_op jit(solution)/shard_map/ppermute | solution.py:236
  27.0 0.6 %again.1 = bf16[48,1536]{1,0:T(8,128)(2,1)S(1)} custom-call(bf16[48,1024]{1,0:T(8,128)(2,1)S(1)} %get-tuple-element.25.sent_ref.refs_1_.attended_ref, bf16[512,2560]{1,0:T(8,128)(2,1)S(1)} %get-tuple-element.24.own_part_ref, bf16[512,2560]{1,0:T(8,128)(2,1)S(1)} %get-tuple-element.33.sib_part_ref), custom_call_target="tpu_custom_call" | custom-call | tf_op jit(solution)/shard_map/again/pallas_call | solution.py:320
  27.6 1.6 %collective-permute-start.12 = (bf16[48,1536]{1,0:T(8,128)(2,1)S(1)}, bf16[48,1536]{1,0:T(8,128)(2,1)S(1)}, u32[]{:S(2)}, u32[]{:S(2)}) collective-permute-start(bf16[48,1536]{1,0:T(8,128)(2,1)S(1)} %again.1), channel_id=1, source_target_pairs={{0,2},{1,3},{2,0},{3,1},{4,6},{5,7},{6,4},{7,5},{8,10},{9,11},{10,... | collective-permute-start | bytes 442376 | tf_op jit(solution)/shard_map/ppermute | solution.py:236
  29.2 2.2 %shard_map.56 = (bf16[48,1536]{1,0:T(8,128)(2,1)S(1)}, bf16[48,1536]{1,0:T(8,128)(2,1)S(1)}) custom-call(bf16[512,8192]{1,0:T(8,128)(2,1)} %own_w_ref.7, bf16[512,8192]{1,0:T(8,128)(2,1)} %collective-permute-done.sib_w_ref, bf16[48,1024]{1,0:T(8,128)(2,1)S(1)} %get-tuple-element.26.refs_0_.attended_ref, ...), custom_call_target="tpu_custom_call" | custom-call | tf_op jit(solution)/shard_map/pallas_call | solution.py:292
  31.4 0.6 %collective-permute-start.9 = (bf16[48,1536]{1,0:T(8,128)(2,1)S(1)}, bf16[48,1536]{1,0:T(8,128)(2,1)S(1)}, u32[]{:S(2)}, u32[]{:S(2)}) collective-permute-start(bf16[48,1536]{1,0:T(8,128)(2,1)S(1)} %get-tuple-element.28), channel_id=1, source_target_pairs={{0,2},{1,3},{2,0},{3,1},{4,6},{5,7},{6,4},{7,5},{8,10},{9,11},{10,... | collective-permute-start | bytes 442376 | tf_op jit(solution)/shard_map/ppermute | solution.py:236
  32.0 1.5 %collective-permute-start.13 = (bf16[48,1024]{1,0:T(8,128)(2,1)S(1)}, bf16[48,1024]{1,0:T(8,128)(2,1)S(1)}, u32[]{:S(2)}, u32[]{:S(2)}) collective-permute-start(bf16[48,1024]{1,0:T(8,128)(2,1)S(1)} %get-tuple-element.36), channel_id=1, source_target_pairs={{0,2},{1,3},{2,0},{3,1},{4,6},{5,7},{6,4},{7,5},{8,10},{9,11},{10,... | collective-permute-start | bytes 294920 | tf_op jit(solution)/shard_map/ppermute | solution.py:236
  33.5 1.0 %rest.1 = (bf16[48,1024]{1,0:T(8,128)(2,1)S(1)}, bf16[48,1536]{1,0:T(8,128)(2,1)S(1)}) custom-call(bf16[48,1024]{1,0:T(8,128)(2,1)S(1)} %get-tuple-element.26.refs_0_.attended_ref, bf16[512,2560]{1,0:T(8,128)(2,1)S(1)} %get-tuple-element.24.own_part_ref, bf16[512,2560]{1,0:T(8,128)(2,1)S(1)} %get-tuple-element.33.sib_part_ref), custom_call_target="tpu_custom_call" | custom-call | tf_op jit(solution)/shard_map/rest/pallas_call | solution.py:346
  34.5 7.6 %collective-permute-done.13.refs_1_ = bf16[48,1024]{1,0:T(8,128)(2,1)S(1)} collective-permute-done((bf16[48,1024]{1,0:T(8,128)(2,1)S(1)}, bf16[48,1024]{1,0:T(8,128)(2,1)S(1)}, u32[]{:S(2)}, u32[]{:S(2)}) %collective-permute-start.13) | collective-permute-done | bytes 98336 | tf_op jit(solution)/shard_map/ppermute | solution.py:236
  42.1 0.7 %finish.5.refs_2_ = bf16[48,8192]{1,0:T(8,128)(2,1)} custom-call(bf16[48,1024]{1,0:T(8,128)(2,1)S(1)} %get-tuple-element.35.refs_0_, bf16[48,1024]{1,0:T(8,128)(2,1)S(1)} %collective-permute-done.13.refs_1_), custom_call_target="tpu_custom_call" | custom-call | tf_op jit(solution)/shard_map/finish/pallas_call | solution.py:355
  42.8 0.0 collective-permute-done.12.refs_1_
  42.8 0.7 %finish.6.refs_2_ = bf16[48,8192]{1,0:T(8,128)(2,1)} custom-call(bf16[48,1536]{1,0:T(8,128)(2,1)S(1)} %get-tuple-element.34.refs_0_, bf16[48,1536]{1,0:T(8,128)(2,1)S(1)} %collective-permute-done.12.refs_1_, bf16[48,8192]{1,0:T(8,128)(2,1)} %finish.5.refs_2_), custom_call_target="tpu_custom_call", output_to_operand_aliasing={{}: (2, {})} | custom-call | tf_op jit(solution)/shard_map/finish/pallas_call | solution.py:355
  43.5 0.0 collective-permute-done.11.refs_1_
  43.6 0.7 %finish.7.refs_2_ = bf16[48,8192]{1,0:T(8,128)(2,1)} custom-call(bf16[48,2048]{1,0:T(8,128)(2,1)S(1)} %get-tuple-element.31.refs_0_, bf16[48,2048]{1,0:T(8,128)(2,1)S(1)} %collective-permute-done.11.refs_1_, bf16[48,8192]{1,0:T(8,128)(2,1)} %finish.6.refs_2_), custom_call_target="tpu_custom_call", output_to_operand_aliasing={{}: (2, {})} | custom-call | tf_op jit(solution)/shard_map/finish/pallas_call | solution.py:355
  44.3 0.0 collective-permute-done.10.refs_1_
  44.3 0.7 %finish.8.refs_2_ = bf16[48,8192]{1,0:T(8,128)(2,1)} custom-call(bf16[48,2048]{1,0:T(8,128)(2,1)S(1)} %get-tuple-element.29.refs_0_, bf16[48,2048]{1,0:T(8,128)(2,1)S(1)} %collective-permute-done.10.refs_1_, bf16[48,8192]{1,0:T(8,128)(2,1)} %finish.7.refs_2_), custom_call_target="tpu_custom_call", output_to_operand_aliasing={{}: (2, {})} | custom-call | tf_op jit(solution)/shard_map/finish/pallas_call | solution.py:355
  45.1 0.0 collective-permute-done.9.refs_1_
  45.1 0.7 %finish.9 = bf16[48,8192]{1,0:T(8,128)(2,1)} custom-call(bf16[48,1536]{1,0:T(8,128)(2,1)S(1)} %get-tuple-element.27.refs_0_, bf16[48,1536]{1,0:T(8,128)(2,1)S(1)} %collective-permute-done.9.refs_1_, bf16[48,8192]{1,0:T(8,128)(2,1)} %finish.8.refs_2_), custom_call_target="tpu_custom_call", output_to_operand_aliasing={{}: (2, {})} | custom-call | tf_op jit(solution)/shard_map/finish/pallas_call | solution.py:355
  (1 shorter events, 0.0 us)
Async XLA Ops:
  0.0 17.9 %collective-permute-start = (bf16[512,8192]{1,0:T(8,128)(2,1)}, bf16[512,8192]{1,0:T(8,128)(2,1)}, u32[]{:S(2)}, u32[]{:S(2)}) collective-permute-start(bf16[512,8192]{1,0:T(8,128)(2,1)} %own_w_ref.7), channel_id=1, source_target_pairs={{0,1},{1,0},{2,3},{3,2},{4,5},{5,4},{6,7},{7,6},{8,9},{9,8},{10,11... | collective-permute-start | bytes 25165832 | tf_op jit(solution)/shard_map/ppermute | solution.py:236
  1.3 8.9 %collective-permute-start.5 = (bf16[192,256]{1,0:T(8,128)(2,1)S(1)}, bf16[192,256]{1,0:T(8,128)(2,1)S(1)}, u32[]{:S(2)}, u32[]{:S(2)}) collective-permute-start(bf16[192,256]{1,0:T(8,128)(2,1)S(1)} %pad_maximum_fusion.refs_0_), channel_id=1, source_target_pairs={{0,4},{1,5},{2,6},{3,7},{4,0},{5,1},{6,2},{7,3},{8,12},{9,13},{10,... | collective-permute-start | bytes 294920 | tf_op jit(solution)/shard_map/ppermute | solution.py:236
  3.9 7.1 %collective-permute-start.4 = (bf16[192,256]{1,0:T(8,128)(2,1)S(1)}, bf16[192,256]{1,0:T(8,128)(2,1)S(1)}, u32[]{:S(2)}, u32[]{:S(2)}) collective-permute-start(bf16[192,256]{1,0:T(8,128)(2,1)S(1)} %pad_maximum_fusion.refs_0_), channel_id=1, source_target_pairs={{0,24},{1,13},{2,26},{3,15},{4,28},{5,9},{6,30},{7,11},{8,16},{9,5... | collective-permute-start | bytes 294920 | tf_op jit(solution)/shard_map/ppermute | solution.py:236
  7.5 5.8 %collective-permute-start.3 = (bf16[192,256]{1,0:T(8,128)(2,1)S(1)}, bf16[192,256]{1,0:T(8,128)(2,1)S(1)}, u32[]{:S(2)}, u32[]{:S(2)}) collective-permute-start(bf16[192,256]{1,0:T(8,128)(2,1)S(1)} %pad_maximum_fusion.refs_0_), channel_id=1, source_target_pairs={{0,8},{1,29},{2,10},{3,31},{4,12},{5,25},{6,14},{7,27},{8,0},{9,21... | collective-permute-start | bytes 294920 | tf_op jit(solution)/shard_map/ppermute | solution.py:236
  7.5 9.1 %collective-permute-start.2 = (bf16[192,256]{1,0:T(8,128)(2,1)S(1)}, bf16[192,256]{1,0:T(8,128)(2,1)S(1)}, u32[]{:S(2)}, u32[]{:S(2)}) collective-permute-start(bf16[192,256]{1,0:T(8,128)(2,1)S(1)} %pad_maximum_fusion.refs_0_), channel_id=1, source_target_pairs={{0,16},{1,21},{2,18},{3,23},{4,20},{5,17},{6,22},{7,19},{8,24},{9,... | collective-permute-start | bytes 294920 | tf_op jit(solution)/shard_map/ppermute | solution.py:236
  10.2 6.8 %collective-permute-start.1 = (bf16[96,512]{1,0:T(8,128)(2,1)S(1)}, bf16[96,512]{1,0:T(8,128)(2,1)S(1)}, u32[]{:S(2)}, u32[]{:S(2)}) collective-permute-start(bf16[96,512]{1,0:T(8,128)(2,1)S(1)} %get-tuple-element.23), channel_id=1, source_target_pairs={{0,1},{1,0},{2,3},{3,2},{4,5},{5,4},{6,7},{7,6},{8,9},{9,8},{10,11... | collective-permute-start | bytes 294920 | tf_op jit(solution)/shard_map/ppermute | solution.py:236
  11.0 6.0 %collective-permute-start.8 = (bf16[192,256]{1,0:T(8,128)(2,1)S(1)}, bf16[192,256]{1,0:T(8,128)(2,1)S(1)}, u32[]{:S(2)}, u32[]{:S(2)}) collective-permute-start(bf16[192,256]{1,0:T(8,128)(2,1)S(1)} %collective-permute-done.4.refs_3_), channel_id=1, source_target_pairs={{0,1},{1,0},{2,3},{3,2},{4,5},{5,4},{6,7},{7,6},{8,9},{9,8},{10,11... | collective-permute-start | bytes 294920 | tf_op jit(solution)/shard_map/ppermute | solution.py:236
  13.3 3.7 %collective-permute-start.7 = (bf16[192,256]{1,0:T(8,128)(2,1)S(1)}, bf16[192,256]{1,0:T(8,128)(2,1)S(1)}, u32[]{:S(2)}, u32[]{:S(2)}) collective-permute-start(bf16[192,256]{1,0:T(8,128)(2,1)S(1)} %collective-permute-done.3.refs_2_), channel_id=1, source_target_pairs={{0,1},{1,0},{2,3},{3,2},{4,5},{5,4},{6,7},{7,6},{8,9},{9,8},{10,11... | collective-permute-start | bytes 294920 | tf_op jit(solution)/shard_map/ppermute | solution.py:236
  16.6 1.3 %collective-permute-start.6 = (bf16[192,256]{1,0:T(8,128)(2,1)S(1)}, bf16[192,256]{1,0:T(8,128)(2,1)S(1)}, u32[]{:S(2)}, u32[]{:S(2)}) collective-permute-start(bf16[192,256]{1,0:T(8,128)(2,1)S(1)} %collective-permute-done.2.refs_1_), channel_id=1, source_target_pairs={{0,1},{1,0},{2,3},{3,2},{4,5},{5,4},{6,7},{7,6},{8,9},{9,8},{10,11... | collective-permute-start | bytes 294920 | tf_op jit(solution)/shard_map/ppermute | solution.py:236
  22.3 21.3 %collective-permute-start.11 = (bf16[48,2048]{1,0:T(8,128)(2,1)S(1)}, bf16[48,2048]{1,0:T(8,128)(2,1)S(1)}, u32[]{:S(2)}, u32[]{:S(2)}) collective-permute-start(bf16[48,2048]{1,0:T(8,128)(2,1)S(1)} %get-tuple-element.32), channel_id=1, source_target_pairs={{0,2},{1,3},{2,0},{3,1},{4,6},{5,7},{6,4},{7,5},{8,10},{9,11},{10,... | collective-permute-start | bytes 589832 | tf_op jit(solution)/shard_map/ppermute | solution.py:236
  26.4 17.9 %collective-permute-start.10 = (bf16[48,2048]{1,0:T(8,128)(2,1)S(1)}, bf16[48,2048]{1,0:T(8,128)(2,1)S(1)}, u32[]{:S(2)}, u32[]{:S(2)}) collective-permute-start(bf16[48,2048]{1,0:T(8,128)(2,1)S(1)} %get-tuple-element.30), channel_id=1, source_target_pairs={{0,2},{1,3},{2,0},{3,1},{4,6},{5,7},{6,4},{7,5},{8,10},{9,11},{10,... | collective-permute-start | bytes 589832 | tf_op jit(solution)/shard_map/ppermute | solution.py:236
  27.6 15.2 %collective-permute-start.12 = (bf16[48,1536]{1,0:T(8,128)(2,1)S(1)}, bf16[48,1536]{1,0:T(8,128)(2,1)S(1)}, u32[]{:S(2)}, u32[]{:S(2)}) collective-permute-start(bf16[48,1536]{1,0:T(8,128)(2,1)S(1)} %again.1), channel_id=1, source_target_pairs={{0,2},{1,3},{2,0},{3,1},{4,6},{5,7},{6,4},{7,5},{8,10},{9,11},{10,... | collective-permute-start | bytes 442376 | tf_op jit(solution)/shard_map/ppermute | solution.py:236
  31.4 13.6 %collective-permute-start.9 = (bf16[48,1536]{1,0:T(8,128)(2,1)S(1)}, bf16[48,1536]{1,0:T(8,128)(2,1)S(1)}, u32[]{:S(2)}, u32[]{:S(2)}) collective-permute-start(bf16[48,1536]{1,0:T(8,128)(2,1)S(1)} %get-tuple-element.28), channel_id=1, source_target_pairs={{0,2},{1,3},{2,0},{3,1},{4,6},{5,7},{6,4},{7,5},{8,10},{9,11},{10,... | collective-permute-start | bytes 442376 | tf_op jit(solution)/shard_map/ppermute | solution.py:236
  32.0 10.1 %collective-permute-start.13 = (bf16[48,1024]{1,0:T(8,128)(2,1)S(1)}, bf16[48,1024]{1,0:T(8,128)(2,1)S(1)}, u32[]{:S(2)}, u32[]{:S(2)}) collective-permute-start(bf16[48,1024]{1,0:T(8,128)(2,1)S(1)} %get-tuple-element.36), channel_id=1, source_target_pairs={{0,2},{1,3},{2,0},{3,1},{4,6},{5,7},{6,4},{7,5},{8,10},{9,11},{10,... | collective-permute-start | bytes 294920 | tf_op jit(solution)/shard_map/ppermute | solution.py:236
